TPU v7x, 512 devices: a whole 4x8x8 slice. The times are simulated.
512 devices in a mesh: rep: 8 (over x, core), shard: 64 (over z, y).
Axes of the slice: x: 4, y: 8, z: 8, core: 2. Of those that a mesh axis runs over, the one named last changes fastest.
Arguments:
- features: float32 [262144, 256], P(('rep', 'shard')), may hold values from -6 to 6
- seed_self: float32 [65536, 256], P(('rep', 'shard')), may hold values from -6 to 6
- hub_ids: int32 [65536], P(('rep', 'shard')), may hold values from 0 to 511
- requests: int32 [32768, 32], P(('rep', 'shard')), may hold values from 0 to 511
- counts: int32 [32768], P(('rep', 'shard')), may hold values from 1 to 32, as said below
- neighbors: int32 [65536, 15], P(('rep', 'shard')), may hold values from 0 to 3071
- weight: float32 [256, 256], replicated, may hold values from -1 to 1
- out_bias: float32 [256], replicated, may hold values from -4 to 4
Outputs:
- embedded: float32 [65536, 256], P(('rep', 'shard'))
Inputs may be any that keep to these rules, and one draw needn't show every extreme that they name: `hub_ids`: offsets into the block of features of the same device. `requests`: row d of a device's lists holds offsets into the block of features of the device at shard index d with the same rep index; empty slots hold offsets too. counts[r, s, d] slots of the list from shard index s to shard index d are live, the first ones; for every rep index some destination has 32 live slots from every source. `neighbors`: A code below 1024 names a row of the device's hub cache; a code 1024 + d * 32 + c names slot c of the device's list to shard index d, and counts only where that slot is live.
All inputs are finite; a program needn't handle non-finite values.
Results may differ from a plain program's by a relative error of at most 0.0003.
Values sent between devices are 32-bit elements; how exact they have to be, the bound alone decides.
A program may use at most 64 MiB of HBM per device.

v0:
```python
import math

import jax
import jax.numpy as jnp
from jax import lax
from jax.sharding import Mesh
from jax.sharding import PartitionSpec as P

REP = ("rep_0", "rep_1")
REP_SHARD = ("rep_0", "rep_1", "shard")


def edges_of(length, count):
    turn = length // count
    if turn >= 8:
        turn -= turn % 8
    return [turn * k for k in range(1, count)]


def all_blocks(x, axes, sequence):
    tiles = x
    for k in sequence:
        tiles = lax.all_gather(tiles, axes[k])
    done = sequence[::-1]
    back = [done.index(k) for k in range(len(axes))]
    tiles = tiles.transpose(*back, *range(len(axes), tiles.ndim))
    return tiles.reshape(-1, *x.shape)


def in_order(tiles, dim):
    shape = list(tiles.shape[1:])
    shape[dim] *= tiles.shape[0]
    return jnp.moveaxis(tiles, 0, dim).reshape(shape)


def gather_all_axes(x, axes, dim):
    numbers = list(range(len(axes)))[::-1]
    cut = x.shape.index(max(x.shape[:-1] or x.shape))
    edges = [0, *edges_of(x.shape[cut], len(axes)), x.shape[cut]]
    gathered = []
    for k, (start, end) in enumerate(zip(edges, edges[1:])):
        if end > start:
            piece = lax.slice_in_dim(x, start, end, axis=cut)
            gathered.append(all_blocks(piece, axes, numbers[k:] + numbers[:k]))
    return in_order(jnp.concatenate(gathered, axis=cut + 1), dim)


def count_product(rows, codes, offset, row_scale):
    seed_count, fanout = codes.shape
    block_size = math.gcd(seed_count, 128)
    row_count = rows.shape[0]
    code_iota = lax.broadcasted_iota(jnp.int32, (1, row_count), 1) + offset

    def per_block(block_codes):
        tally = jnp.zeros((block_size, row_count), jnp.float32)
        for column in range(fanout):
            tally = tally + (block_codes[:, column : column + 1] == code_iota).astype(jnp.float32)
        tally = tally * row_scale[None, :]
        return jnp.dot(
            tally, rows, precision=lax.Precision.HIGHEST, preferred_element_type=jnp.float32
        )

    summed = lax.map(per_block, codes.reshape(-1, block_size, fanout))
    return summed.reshape(seed_count, rows.shape[1])


def project(values, weight):
    return jnp.dot(
        values, weight, precision=lax.Precision.HIGHEST, preferred_element_type=jnp.float32
    )


def local(features, seed_self, hub_ids, requests, counts, neighbors, weight, out_bias):
    shard_count = lax.axis_size("shard")
    capacity = requests.shape[1]
    feat_width = features.shape[1]
    hub_total = hub_ids.shape[0] * lax.axis_size(REP)
    local_hubs = jnp.take(features, hub_ids, axis=0)
    slot_index = lax.broadcasted_iota(jnp.int32, (shard_count, capacity), 1)
    slot_live = (slot_index < counts[:, None]).astype(jnp.float32).reshape(-1)
    code_live = jnp.concatenate([jnp.ones((hub_total,), jnp.float32), slot_live])
    weights = jnp.take(code_live, neighbors)
    taken = 1.0 + jnp.sum(weights, axis=1)
    hub_rows = gather_all_axes(local_hubs, REP, 0)
    hub_part = count_product(hub_rows, neighbors, 0, jnp.ones((hub_total,), jnp.float32))
    looked = jnp.take(
        features, lax.all_to_all(requests, "shard", split_axis=0, concat_axis=0, tiled=True), axis=0
    )
    fetched = lax.all_to_all(looked, "shard", split_axis=0, concat_axis=0, tiled=True)
    slot_rows = fetched.reshape(-1, feat_width)
    slot_part = count_product(slot_rows, neighbors, hub_total, slot_live)
    total = seed_self + (hub_part + slot_part)
    mean_rows = total / taken[:, None]
    product = project(mean_rows, weight)
    return jnp.maximum(product + out_bias, 0.0)


def solution(mesh):
    finer = Mesh(mesh.devices.reshape(4, 2, mesh.shape["shard"]), ("rep_0", "rep_1", "shard"))
    in_specs = (
        P(REP_SHARD, None),
        P(REP_SHARD, None),
        P(REP_SHARD),
        P(REP_SHARD, None),
        P(REP_SHARD),
        P(REP_SHARD, None),
        P(),
        P(),
    )
    out_specs = P(REP_SHARD, None)
    return jax.shard_map(local, mesh=finer, in_specs=in_specs, out_specs=out_specs, check_vma=False)
```

profile of v0, /device:TPU:6, one launch (start us, length us, event | category | flops | bytes accessed | tf_op | source)
XLA Modules:
  0.0 98.2 jit_solution(12739153385083418009)
XLA Ops:
  0.0 0.0 copy-start
  0.0 0.9 copy.27
  0.9 28.4 %all_to_all.20 = s32[64,1,32]{2,1,0:T(1,128)S(1)} all-to-all(s32[64,1,32]{2,1,0:T(1,128)S(1)} %bitcast.57), channel_id=1, replica_groups=mesh['rep_0'=4,'rep_1'=2,'shard'=64] {'shard'}, dimensions={0} | all-to-all | bytes 16384 | tf_op jit(solution)/shard_map/all_to_all | solution.py:87
  29.3 0.1 reshape.111
  29.4 0.0 copy-done
  29.4 6.6 %gather_fusion.1 = f32[2048,256]{1,0:T(8,128)S(1)} fusion(f32[512,256]{1,0:T(8,128)S(1)} %copy-done, s32[2048]{0:T(1024)S(1)} %broadcast_clamp_fusion), kind=kCustom, calls=%fused_computation.1 | custom fusion | bytes 4202496 | tf_op jit(solution)/shard_map/jit(_take)/gather | solution.py:86
  36.0 1.7 %broadcast_select_fusion = f32[64,32,256]{2,1,0:T(8,128)} fusion(f32[64,32,256]{2,1,0:T(8,128)S(1)} %bitcast.48, pred[64,32]{1,0:T(8,128)(4,1)S(1)} %compare_and_fusion), kind=kLoop, calls=%fused_computation.9 | loop fusion | flops 524288 | bytes 4196352 | tf_op jit(solution)/shard_map/jit(_take)/select_n | solution.py:86
  37.7 4.8 %all-to-all-start.1 = ((f32[64,32,256]{2,1,0:T(8,128)}), f32[64,32,256]{2,1,0:T(8,128)S(1)}, u32[]{:S(2)}, u32[]{:S(2)}) async-start(f32[64,32,256]{2,1,0:T(8,128)} %broadcast_select_fusion), calls=%async_computation.1 | async-start | bytes 4194304 | tf_op jit(solution)/shard_map/all_to_all | solution.py:89
  42.5 0.0 copy-done.6
  42.6 0.0 copy-start.4
  42.6 0.0 copy-start.2
  42.6 0.8 gather_fusion
  43.4 0.1 broadcast_select_fusion.1
  43.5 12.3 %all-gather.2 = f32[256,256]{1,0:T(8,128)S(1)} all-gather(f32[64,256]{1,0:T(8,128)S(1)} %get-tuple-element.25), channel_id=4, replica_groups=mesh['rep_0'=4,'rep_1'=2,'shard'=64] {'rep_0'}, dimensions={0}, use_global_device_ids=true | all-gather | bytes 327680 | tf_op jit(solution)/shard_map/all_gather | solution.py:23
  55.7 2.2 %all-gather.3 = f32[8,64,256]{2,1,0:T(8,128)S(1)} all-gather(f32[4,64,256]{2,1,0:T(8,128)S(1)} %bitcast.52), channel_id=5, replica_groups=mesh['rep_0'=4,'rep_1'=2,'shard'=64] {'rep_1'}, dimensions={0}, use_global_device_ids=true | all-gather | bytes 786432 | tf_op jit(solution)/shard_map/all_gather | solution.py:23
  58.0 0.0 copy-done.4
  58.0 0.1 fusion.110
  58.0 0.1 reshape.100
  58.1 0.0 copy-done.2
  58.1 0.1 copy.28
  58.2 0.2 reshape.119
  58.5 10.4 %gather_fusion.2 = f32[1920]{0:T(1024)S(1)} fusion(f32[3072]{0:T(1024)S(1)} %concatenate.7, s32[2048]{0:T(1024)S(1)} %pad_clamp_fusion), kind=kCustom, calls=%fused_computation.2 | custom fusion | bytes 23040 | tf_op jit(solution)/shard_map/jit(_take)/gather | solution.py:82
  68.9 0.2 reshape.118
  69.1 0.1 copy.29
  69.1 1.9 %all-gather = f32[128,256]{1,0:T(8,128)S(1)} all-gather(f32[64,256]{1,0:T(8,128)S(1)} %get-tuple-element.24), channel_id=2, replica_groups=mesh['rep_0'=4,'rep_1'=2,'shard'=64] {'rep_1'}, dimensions={0}, use_global_device_ids=true | all-gather | bytes 196608 | tf_op jit(solution)/shard_map/all_gather | solution.py:23
  71.1 12.8 %all-gather.1 = f32[8,64,256]{2,1,0:T(8,128)S(1)} all-gather(f32[2,64,256]{2,1,0:T(8,128)S(1)} %bitcast.54), channel_id=3, replica_groups=mesh['rep_0'=4,'rep_1'=2,'shard'=64] {'rep_0'}, dimensions={0}, use_global_device_ids=true | all-gather | bytes 655360 | tf_op jit(solution)/shard_map/all_gather | solution.py:23
  83.9 0.1 pad_maximum_fusion
  83.9 0.0 copy-start.5
  84.0 2.3 %fusion.50 = f32[128,256]{1,0:T(8,128)S(1)} fusion(f32[1024,256]{1,0:T(8,128)S(1)} %bitcast.53, s32[128]{0:T(128)S(1)} %get-tuple-element.54, s32[128]{0:T(128)S(1)} %get-tuple-element.33, s32[128]{0:T(128)S(1)} %get-tuple-element.34, s32[128]{0:T(128)S(1)} %get-tuple-element.35, s32[128]{0:T(128)S(1)} %get-tuple-element.36, s32[128]{0:T(128)S(1)} %get-tuple-element.37, ...), kind=kOutput, calls=%fused_computation.57 | convolution fusion | flops 408420352 | bytes 1187328 | tf_op jit(solution)/shard_map/while/body/eval_jaxpr/dot_general | solution.py:59
  86.3 8.1 %all-to-all-done.1 = f32[64,32,256]{2,1,0:T(8,128)S(1)} async-done(((f32[64,32,256]{2,1,0:T(8,128)}), f32[64,32,256]{2,1,0:T(8,128)S(1)}, u32[]{:S(2)}, u32[]{:S(2)}) %all-to-all-start.1) | async-done | bytes 2097184 | tf_op jit(solution)/shard_map/all_to_all | solution.py:89
  94.4 2.7 %fusion.2 = f32[128,256]{1,0:T(8,128)S(1)} fusion(f32[128,256]{1,0:T(8,128)S(1)} %copy-done.5, f32[128,256]{1,0:T(8,128)S(1)} %fusion.50, f32[2048,256]{1,0:T(8,128)S(1)} %bitcast.49, f32[2048]{0:T(1024)S(1)} %reshape.100, s32[2048]{0:T(1024)S(1)} %iota_add_fusion, s32[128]{0:T(128)S(1)} %get-tuple-element.54, s32[128]{0:T(128)S(1)} %get-tuple-element.33, ...), kind=kOutput, calls=%fused_computation.7 | convolution fusion | flops 817201152 | bytes 2514944 | tf_op jit(solution)/shard_map/while/body/eval_jaxpr/dot_general | solution.py:59
  97.2 0.9 fusion
  (21 shorter events, 0.2 us)
Async XLA Ops:
  0.0 29.4 %copy-start = (f32[512,256]{1,0:T(8,128)S(1)}, f32[512,256]{1,0:T(8,128)}, u32[]{:S(2)}) copy-start(f32[512,256]{1,0:T(8,128)} %param.8) | copy-start | bytes 1572868
  37.7 4.8 %copy-start.6 = (s32[128]{0:T(128)S(1)}, s32[128]{0:T(128)}, u32[]{:S(2)}) copy-start(s32[128]{0:T(128)} %param.10) | copy-start | bytes 1540
  37.7 56.7 %all-to-all-start.1 = ((f32[64,32,256]{2,1,0:T(8,128)}), f32[64,32,256]{2,1,0:T(8,128)S(1)}, u32[]{:S(2)}, u32[]{:S(2)}) async-start(f32[64,32,256]{2,1,0:T(8,128)} %broadcast_select_fusion), calls=%async_computation.1 | async-start | bytes 4194304 | tf_op jit(solution)/shard_map/all_to_all | solution.py:89
  42.6 15.4 %copy-start.4 = (s32[64]{0:T(128)S(1)}, s32[64]{0:T(128)}, u32[]{:S(2)}) copy-start(s32[64]{0:T(128)} %param.12) | copy-start | bytes 772
  42.6 15.6 %copy-start.2 = (s32[128,15]{0,1:T(8,128)S(1)}, s32[128,15]{0,1:T(8,128)}, u32[]{:S(2)}) copy-start(s32[128,15]{0,1:T(8,128)} %param.13) | copy-start | bytes 23044
  83.9 10.5 %copy-start.5 = (f32[128,256]{1,0:T(8,128)S(1)}, f32[128,256]{1,0:T(8,128)}, u32[]{:S(2)}) copy-start(f32[128,256]{1,0:T(8,128)} %param.9) | copy-start | bytes 393220
  94.4 2.8 %copy-start.1 = (f32[256,256]{1,0:T(8,128)S(1)}, f32[256,256]{1,0:T(8,128)}, u32[]{:S(2)}) copy-start(f32[256,256]{1,0:T(8,128)} %param.14) | copy-start | bytes 786436
  94.4 2.8 %copy-start.3 = (f32[256]{0:T(256)S(1)}, f32[256]{0:T(256)}, u32[]{:S(2)}) copy-start(f32[256]{0:T(256)} %param.15) | copy-start | bytes 3076
where the time goes:
time: 98.4 us; the launch traced here: 98.2 us
  blocking collectives  57.5 us (58%)
  local copies, waits for them, and re-layouts  19.5 us (20%)
  waiting for transfers between devices  8.14 us (8%)
  matrix products  5.99 us (6%)
  starting transfers between devices  4.82 us (5%)
  other arithmetic  2 us (2%)
    all_gather x4, blocking collectives, all_blocks(): tiles = lax.all_gather(tiles, axes[k])  29.1 us
    all_to_all x1, blocking collectives, local(): lax.all_to_all(requests, 'shard', split_axis=0, concat_axis=0, tiled=True)  28.4 us
    gather x3, local copies, waits for them, and re-layouts, local(): weights = jnp.take(code_live, neighbors)  10.7 us
    all_to_all x1, waiting for transfers between devices, local(): lax.all_to_all(looked, 'shard', split_axis=0, concat_axis=0, tiled=True)  8.14 us
    gather x1, local copies, waits for them, and re-layouts, local(): jnp.take(features, lax.all_to_all(requests, 'shard', split_axis=0, concat...  6.64 us
    dot_general x2, matrix products, per_block(): jnp.dot(tally, rows, precision=lax.Precision.HIGHEST, preferred_element_t...  5.05 us
    all_to_all x1, starting transfers between devices, local(): lax.all_to_all(looked, 'shard', split_axis=0, concat_axis=0, tiled=True)  4.82 us
  transfers between devices with their start and end apart: 1, of which 1 were waited for; matrix products, arithmetic and copies ran while one was open for 15% of the time, Pallas kernels for 0%

commit v1 on v0

v1 whole, which is shorter than its diff:
```python
import functools

import jax
import jax.numpy as jnp
from jax import lax
from jax.experimental import pallas as pl
from jax.experimental.pallas import tpu as pltpu
from jax.sharding import PartitionSpec as P

MESH = pl.DeviceIdType.MESH
RING = 8
XS = 4
ROWS = 512
SEEDS = 128
FAN = 15
CAP = 32
HUBS = 1024
CHUNKS = 4
LANES = 128


def split(values):
    high = values.astype(jnp.bfloat16)
    low = (values - high.astype(jnp.float32)).astype(jnp.bfloat16)
    return jnp.concatenate([high, low], axis=0)


def dot(left, right):
    return jnp.dot(left, right, preferred_element_type=jnp.float32)


def kernel(
    feat, own, hub_id, req, req_t, counts, codes_t, weight, bias, out,
    ag, meta_tx, meta_rx, ids, cblk, gacc, pacc, part, hubs, tot, taken,
    ag_send, ag_recv, meta_send, meta_recv, part_send, part_recv, hub_send, hub_recv,
):
    rep = lax.axis_index("rep")
    shard = lax.axis_index("shard")
    me_x, core = rep // 2, rep % 2
    me = (shard % RING, shard // RING)

    def along_y(step):
        return {"rep": rep, "shard": me[1] * RING + (me[0] + step) % RING}

    def along_z(step):
        return {"rep": rep, "shard": ((me[1] + step) % RING) * RING + me[0]}

    def along_x(step):
        return {"rep": ((me_x + step) % XS) * 2 + core, "shard": shard}

    ring = (along_y, along_z)
    cross = (along_z, along_y)
    spot = (me[1], me[0])

    barrier = pltpu.get_barrier_semaphore()
    peers = [along_y(d) for d in range(1, RING)] + [along_z(d) for d in range(1, RING)]
    partner = {"rep": me_x * 2 + 1 - core, "shard": shard}
    peers += [partner, along_x(1), along_x(XS - 1)]
    for peer in peers:
        pl.semaphore_signal(barrier, inc=1, device_id=peer, device_id_type=MESH)

    def push(src, dst, send, recv, peer):
        return pltpu.make_async_remote_copy(
            src_ref=src, dst_ref=dst, send_sem=send, recv_sem=recv, device_id=peer, device_id_type=MESH
        )

    for half in range(2):
        for chunk in range(CHUNKS):
            block = feat[chunk * LANES : (chunk + 1) * LANES, half * LANES : (half + 1) * LANES]
            ag[half, 0, chunk] = jnp.transpose(block)

    codes = codes_t[...]
    owner = (codes - HUBS) >> 5
    slot = (codes - HUBS) & 31

    def look(d, found):
        return jnp.where(owner == d, counts[d], found)

    filled = lax.fori_loop(0, RING * RING, look, jnp.zeros_like(codes), unroll=8)
    live = (codes >= 0) & ((codes < HUBS) | (slot < filled))
    codes = jnp.where(live, codes, -1)
    taken[...] = 1.0 + jnp.sum(live.astype(jnp.float32), axis=0, keepdims=True)
    for half, source in enumerate((req, req_t)):
        turned = pltpu.roll(source[...], (spot[half] % 4) * CAP, 1)
        for place in range(RING):
            meta_tx[half, place, 0:16] = codes
            meta_tx[half, place, 16:24] = turned[place * RING : (place + 1) * RING]
        meta_rx[half, spot[half], 0:16] = codes
    for half in range(2):
        meta_rx[half, spot[half], 16:24] = meta_tx[half, spot[half], 16:24]

    hub_sum = jnp.zeros((4 * LANES, LANES), jnp.float32)
    for chunk in range(CHUNKS):
        block = jnp.concatenate([ag[0, 0, chunk], ag[1, 0, chunk]], axis=0)
        rows = lax.broadcasted_iota(jnp.int32, (LANES, LANES), 0) + chunk * LANES
        pick = jnp.where(rows == hub_id[...], 1.0, 0.0).astype(jnp.bfloat16)
        hub_sum = hub_sum + dot(split(block), pick)
    hubs[0] = hub_sum[: 2 * LANES] + hub_sum[2 * LANES :]

    pl.semaphore_wait(barrier, len(peers))

    sent = []

    def launch(copy):
        copy.start()
        sent.append(copy)

    metas = []
    for step in (4, 3, 5, 2, 6, 1, 7):
        for half in range(2):
            place = (spot[half] + step) % RING
            copy = push(
                meta_tx.at[half, place], meta_rx.at[half, spot[half]],
                meta_send.at[half, step - 1], meta_recv.at[half, step - 1], cross[half](step),
            )
            launch(copy)
            metas.append(copy)

    def table(half, way, wave, chunk):
        slot_from = wave if way == 0 else (RING - wave) % RING
        slot_to = wave + 1 if way == 0 else RING - wave - 1
        return push(
            ag.at[half, slot_from, chunk], ag.at[half, slot_to, chunk],
            ag_send.at[half, way, wave, chunk], ag_recv.at[half, slot_to, chunk],
            ring[half](1 if way == 0 else RING - 1),
        )

    moves = {}
    for chunk in range(CHUNKS):
        for half in range(2):
            for way in range(2):
                moves[half, way, 0, chunk] = table(half, way, 0, chunk)
                launch(moves[half, way, 0, chunk])

    def hub_push(index, src, dst, peer):
        copy = push(src, dst, hub_send.at[index], hub_recv.at[index], peer)
        launch(copy)
        return copy

    hub_right = hub_push(0, hubs.at[0], hubs.at[2], along_x(1))
    hub_left = hub_push(1, hubs.at[0], hubs.at[6], along_x(XS - 1))
    hub_over = [hub_push(2, hubs.at[0], hubs.at[1], partner)]

    cblk[...] = jnp.zeros_like(cblk)
    pacc[...] = jnp.zeros_like(pacc)
    tot[...] = jnp.transpose(own[...])

    for copy in metas:
        copy.wait_recv()
    for half in range(2):
        for group in range(2):
            tiles = [meta_rx[half, 4 * group + k, 16:24] for k in range(4)]
            ids[half, :, group * LANES : (group + 1) * LANES] = tiles[0] + tiles[1] + tiles[2] + tiles[3]

    def place_of(half, slot_index):
        mine = me[0] * (1 - half) + me[1] * half
        return (mine + RING - slot_index) % RING

    def pick_rows(half, slot_index, part_index):
        pieces = [ag[half, slot_index, 2 * part_index + k] for k in range(2)]
        block = split(jnp.concatenate(pieces, axis=1))
        wanted = ids[half, pl.ds(place_of(half, slot_index), 1), :]
        rows = lax.broadcasted_iota(jnp.int32, (2 * LANES, 2 * LANES), 0) + 2 * LANES * part_index
        return dot(block, jnp.where(rows == wanted, 1.0, 0.0).astype(jnp.bfloat16))

    def add_seeds(half, slot_index, rows):
        origin = place_of(half, slot_index)
        number = origin * (1 + half * (RING - 1)) + (me[1] * RING) * (1 - half) + me[0] * half
        lines = lax.broadcasted_iota(jnp.int32, (CAP, LANES), 0) + (HUBS + number * CAP)
        for place in range(RING):
            count = jnp.zeros((CAP, LANES), jnp.float32)
            for k in range(FAN):
                count = count + jnp.where(meta_rx[half, place, k : k + 1] == lines, 1.0, 0.0)
            top, left = CAP * (place % 4), LANES * (place % 2)
            cblk[place // 2, top : top + CAP, left : left + LANES] = count.astype(jnp.bfloat16)
        rows = rows.astype(jnp.bfloat16)
        for pair in range(RING // 2):
            side = (pair // 2) * LANES
            sums = dot(rows[:, side : side + LANES], cblk[pair])
            sums = sums[:LANES] + sums[LANES:]
            for k in range(2):
                pacc[half, 2 * pair + k] += sums[:, k * LANES : (k + 1) * LANES]

    def own_block(half, carry):
        add_seeds(half, 0, pick_rows(half, 0, 0) + pick_rows(half, 0, 1))
        return carry

    lax.fori_loop(0, 2, own_block, 0)

    def first_part(wave, index, carry):
        half, way = index // 2, index % 2
        slot_index = wave + way * (RING - 2 * wave)
        gacc[index] = pick_rows(half, slot_index, 0)
        return carry

    def second_part(wave, index, carry):
        half, way = index // 2, index % 2
        slot_index = wave + way * (RING - 2 * wave)
        add_seeds(half, slot_index, gacc[index] + pick_rows(half, slot_index, 1))
        return carry

    def hub_block(index, carry):
        chip, over = index // 2, index % 2
        origin = ((me_x + XS - chip) % XS) * 2 + (core + over) % 2
        lines = lax.broadcasted_iota(jnp.int32, (LANES, LANES), 0) + origin * LANES
        mine = spot[0]
        count = jnp.zeros((LANES, LANES), jnp.float32)
        for k in range(FAN):
            count = count + jnp.where(meta_rx[0, mine, k : k + 1] == lines, 1.0, 0.0)
        sums = dot(split(hubs[index]), count.astype(jnp.bfloat16))
        tot[...] += sums[: 2 * LANES] + sums[2 * LANES :]
        return carry

    for wave in range(1, 4):
        for chunk in range(CHUNKS):
            for half in range(2):
                for way in range(2):
                    moves[half, way, wave - 1, chunk].wait_recv()
                    if wave < 3 or chunk // 2 == way:
                        moves[half, way, wave, chunk] = table(half, way, wave, chunk)
                        launch(moves[half, way, wave, chunk])
            if chunk == 1:
                lax.fori_loop(0, 4, functools.partial(first_part, wave), 0)
            if chunk == 3:
                lax.fori_loop(0, 4, functools.partial(second_part, wave), 0)
        if wave == 1:
            hub_right.wait_recv()
            hub_left.wait_recv()
            low, high = pl.ds(0, LANES), pl.ds(LANES, LANES)
            far = [
                hub_push(3, hubs.at[2, low], hubs.at[4, low], along_x(1)),
                hub_push(4, hubs.at[6, high], hubs.at[4, high], along_x(XS - 1)),
            ]
            hub_over.append(hub_push(5, hubs.at[2], hubs.at[3], partner))
            hub_over.append(hub_push(6, hubs.at[6], hubs.at[7], partner))
        if wave == 2:
            for copy in far:
                copy.wait_recv()
            hub_over.append(hub_push(7, hubs.at[4], hubs.at[5], partner))

    for copy in hub_over:
        copy.wait_recv()
    lax.fori_loop(0, 8, hub_block, 0)

    for chunk in (0, 2, 1, 3):
        for half in range(2):
            moves[half, chunk // 2, 3, chunk].wait_recv()

    sums_moves = []
    for half in range(2):
        add_seeds(half, 4, pick_rows(half, 4, 0) + pick_rows(half, 4, 1))
        for step in (4, 3, 5, 2, 6, 1, 7):
            copy = push(
                pacc.at[half, (spot[half] + step) % RING], part.at[half, step - 1],
                part_send.at[half, step - 1], part_recv.at[half, step - 1], cross[half](step),
            )
            launch(copy)
            sums_moves.append((half, step, copy))

    for half in range(2):
        tot[half * LANES : (half + 1) * LANES] += pacc[half, spot[half]]
    for wanted in (1, 7, 2, 6, 3, 5, 4):
        for half, step, copy in sums_moves:
            if step == wanted:
                copy.wait_recv()
                tot[half * LANES : (half + 1) * LANES] += part[half, step - 1]

    mean = jnp.transpose(tot[...] / taken[...])
    product = jnp.dot(mean, weight[...], precision=lax.Precision.HIGHEST, preferred_element_type=jnp.float32)
    out[...] = jnp.maximum(product + bias[...], 0.0)
    for copy in sent:
        copy.wait_send()


def local(features, seed_self, hub_ids, requests, counts, neighbors, weight, out_bias):
    codes_t = jnp.pad(neighbors.T, ((0, 16 - FAN), (0, 0)), constant_values=-1)
    req = jnp.pad(requests, ((0, 0), (0, LANES - CAP)))
    req_t = req.reshape(RING, RING, LANES).transpose(1, 0, 2).reshape(RING * RING, LANES)
    vmem = pl.BlockSpec(memory_space=pltpu.VMEM)
    smem = pl.BlockSpec(memory_space=pltpu.SMEM)
    dma = pltpu.SemaphoreType.DMA
    return pl.pallas_call(
        kernel,
        out_shape=jax.ShapeDtypeStruct((SEEDS, 2 * LANES), jnp.float32),
        in_specs=[vmem] * 5 + [smem] + [vmem] * 3,
        out_specs=vmem,
        scratch_shapes=[
            pltpu.VMEM((2, RING, CHUNKS, LANES, LANES), jnp.float32),
            pltpu.VMEM((2, RING, 24, LANES), jnp.int32),
            pltpu.VMEM((2, RING, 24, LANES), jnp.int32),
            pltpu.VMEM((2, RING, 2 * LANES), jnp.int32),
            pltpu.VMEM((4, LANES, 2 * LANES), jnp.bfloat16),
            pltpu.VMEM((4, 2 * LANES, 2 * LANES), jnp.float32),
            pltpu.VMEM((2, RING, LANES, LANES), jnp.float32),
            pltpu.VMEM((2, RING - 1, LANES, LANES), jnp.float32),
            pltpu.VMEM((2 * XS, 2 * LANES, LANES), jnp.float32),
            pltpu.VMEM((2 * LANES, LANES), jnp.float32),
            pltpu.VMEM((1, LANES), jnp.float32),
            dma((2, 2, 4, CHUNKS)),
            dma((2, RING, CHUNKS)),
            dma((2, RING - 1)),
            dma((2, RING - 1)),
            dma((2, RING - 1)),
            dma((2, RING - 1)),
            dma((8,)),
            dma((8,)),
        ],
        compiler_params=pltpu.CompilerParams(collective_id=0, has_side_effects=True, vmem_limit_bytes=48 * 1024 * 1024),
        name="sage",
    )(features, seed_self, hub_ids.reshape(1, LANES), req, req_t, counts, codes_t, weight, out_bias.reshape(1, 2 * LANES))


def solution(mesh):
    rows, flat = P(("rep", "shard"), None), P(("rep", "shard"))
    return jax.shard_map(
        local, mesh=mesh, in_specs=(rows, rows, flat, rows, flat, rows, P(), P()), out_specs=rows, check_vma=False
    )
```

time: 98.4 us -> 60.6 us (0.62)
  blocking collectives: 57.5 us -> 0 us
  Pallas kernels: 0 us -> 55.8 us
  local copies, waits for them, and re-layouts: 19.5 us -> 4.18 us
  waiting for transfers between devices: 8.14 us -> 0 us
  matrix products: 5.99 us -> 0 us
  starting transfers between devices: 4.82 us -> 0 us
  other arithmetic: 2 us -> 0 us
    pallas_call x0 -> x1, Pallas kernels: none -> 55.8 us  [local(): pl.pallas_call(kernel, out_shape=jax.ShapeDtypeStruct((SEEDS, 2 * LANES),...]
    all_gather x4 -> x0, blocking collectives: 29.1 us -> none  [all_blocks(): tiles = lax.all_gather(tiles, axes[k])]
    all_to_all x1 -> x0, blocking collectives: 28.4 us -> none  [local(): lax.all_to_all(requests, 'shard', split_axis=0, concat_axis=0, tiled=True)]
    gather x5 -> x0, local copies, waits for them, and re-layouts: 18.1 us -> none  [the longest x3 10.7 us: local(): weights = jnp.take(code_live, neighbors)]
    all_to_all x1 -> x0, waiting for transfers between devices: 8.14 us -> none  [local(): lax.all_to_all(looked, 'shard', split_axis=0, concat_axis=0, tiled=True)]
    dot_general x3 -> x0, matrix products: 5.99 us -> none  [the longest x2 5.05 us: per_block(): jnp.dot(tally, rows, precision=lax.Precision.HIGHEST, preferred_element_t...]
    all_to_all x1 -> x0, starting transfers between devices: 4.82 us -> none  [local(): lax.all_to_all(looked, 'shard', split_axis=0, concat_axis=0, tiled=True)]
    unnamed x15 -> x16, local copies, waits for them, and re-layouts: 0.89 us -> 3.42 us
  transfers between devices with their start and end apart: 1 -> 0, of which waited for: 1 -> 0; matrix products, arithmetic and copies ran while one was open for 15% -> 0% of each run, Pallas kernels for 0% -> 0%
where the time goes in v1:
time: 60.6 us; the launch traced here: 60 us
  Pallas kernels  55.8 us (92%)
  local copies, waits for them, and re-layouts  4.18 us (7%)
    pallas_call x1, Pallas kernels, local(): pl.pallas_call(kernel, out_shape=jax.ShapeDtypeStruct((SEEDS, 2 * LANES),...  55.8 us
    unnamed x16, local copies, waits for them, and re-layouts  3.42 us

profile of v1, /device:TPU:6, one launch (start us, length us, event | category | flops | bytes accessed | tf_op | source)
XLA Modules:
  0.0 60.0 jit_solution(17109451195828671650)
XLA Ops:
  0.0 0.0 copy-start.6
  0.0 0.0 copy-start.2
  0.0 0.7 %pad.9.codes_t = s32[16,128]{1,0:T(8,128)S(1)} pad(s32[15,128]{1,0:T(8,128)} %bitcast.13, s32[]{:T(128)} %constant.1.clone.1), padding=0_1x0_0 | pad | bytes 15876 | tf_op jit(solution)/shard_map/jit(_pad)/pad | solution.py:276
  0.7 0.0 copy-done.6
  0.7 0.1 copy.9
  0.8 0.0 copy-start.5
  0.9 0.0 copy-start.3
  0.9 0.0 copy-start.4
  0.9 0.0 copy-done.2
  0.9 0.6 copy-done.5
  1.5 0.1 copy-done.3
  1.6 0.0 copy-done.4
  1.6 0.0 copy-start
  1.6 1.0 %copy-done = f32[512,256]{1,0:T(8,128)S(1)} copy-done((f32[512,256]{1,0:T(8,128)S(1)}, f32[512,256]{1,0:T(8,128)}, u32[]{:S(2)}) %copy-start) | copy-done | bytes 524312
  2.6 0.0 copy-start.1
  2.6 0.9 %copy-done.1 = f32[256,256]{1,0:T(8,128)S(1)} copy-done((f32[256,256]{1,0:T(8,128)S(1)}, f32[256,256]{1,0:T(8,128)}, u32[]{:S(2)}) %copy-start.1) | copy-done | bytes 262168
  3.6 55.8 %sage.1 = f32[128,256]{1,0:T(8,128)S(1)} custom-call(f32[512,256]{1,0:T(8,128)S(1)} %copy-done, f32[128,256]{1,0:T(8,128)S(1)} %copy-done.2, s32[1,128]{1,0:T(1,128)S(1)} %bitcast.12, s32[64,128]{1,0:T(8,128)S(1)} %get-tuple-element.6.req, s32[64,128]{1,0:T(8,128)S(1)} %bitcast.10, s32[64]{0:T(128)S(1)} %copy-done.5, s32[16,128]{1,0:T(8,128)S(1)} %pad.9.codes_t, ...), custom_call_target="tpu_custom_call" | custom-call | tf_op jit(solution)/shard_map/sage/pallas_call | solution.py:282
  59.4 0.7 %copy.14 = f32[128,256]{1,0:T(8,128)} copy(f32[128,256]{1,0:T(8,128)S(1)} %sage.1) | data formatting | bytes 262144
  (2 shorter events, 0.0 us)
Async XLA Ops:
  0.0 0.7 %copy-start.6 = (s32[64,32]{0,1:T(8,128)S(1)}, s32[64,32]{0,1:T(8,128)}, u32[]{:S(2)}) copy-start(s32[64,32]{0,1:T(8,128)} %param.11) | copy-start | bytes 24580
  0.0 0.9 %copy-start.2 = (f32[128,256]{1,0:T(8,128)S(1)}, f32[128,256]{1,0:T(8,128)}, u32[]{:S(2)}) copy-start(f32[128,256]{1,0:T(8,128)} %own.1) | copy-start | bytes 393220
  0.8 0.7 %copy-start.5 = (s32[64]{0:T(128)S(1)}, s32[64]{0:T(128)}, u32[]{:S(2)}) copy-start(s32[64]{0:T(128)} %counts.1) | copy-start | bytes 772
  0.9 0.7 %copy-start.3 = (f32[256]{0:T(256)S(1)}, f32[256]{0:T(256)}, u32[]{:S(2)}) copy-start(f32[256]{0:T(256)} %param.15) | copy-start | bytes 3076
  0.9 0.7 %copy-start.4 = (s32[128]{0:T(128)S(1)}, s32[128]{0:T(128)}, u32[]{:S(2)}) copy-start(s32[128]{0:T(128)} %param.10) | copy-start | bytes 1540
  1.6 1.0 %copy-start = (f32[512,256]{1,0:T(8,128)S(1)}, f32[512,256]{1,0:T(8,128)}, u32[]{:S(2)}) copy-start(f32[512,256]{1,0:T(8,128)} %feat.1) | copy-start | bytes 1572868
  2.6 0.9 %copy-start.1 = (f32[256,256]{1,0:T(8,128)S(1)}, f32[256,256]{1,0:T(8,128)}, u32[]{:S(2)}) copy-start(f32[256,256]{1,0:T(8,128)} %weight.1) | copy-start | bytes 786436

commit v2 on v1

--- a/solution.py
+++ b/solution.py
@@ -30,9 +30,10 @@
 
 
 def kernel(
-    feat, own, hub_id, req, req_t, counts, codes_t, weight, bias, out,
+    feat_in, own_in, hub_in, req_in, counts_in, codes_in, weight_in, bias_in, out,
+    feat, own, hub_id, req_v, req, counts, codes_v, weight, bias, fetch,
     ag, meta_tx, meta_rx, ids, cblk, gacc, pacc, part, hubs, tot, taken,
-    ag_send, ag_recv, meta_send, meta_recv, part_send, part_recv, hub_send, hub_recv,
+    ag_send, ag_recv, meta_send, meta_recv, part_send, part_recv, hub_send, hub_recv, token,
 ):
     rep = lax.axis_index("rep")
     shard = lax.axis_index("shard")
@@ -53,68 +54,33 @@
     spot = (me[1], me[0])
 
     barrier = pltpu.get_barrier_semaphore()
-    peers = [along_y(d) for d in range(1, RING)] + [along_z(d) for d in range(1, RING)]
     partner = {"rep": me_x * 2 + 1 - core, "shard": shard}
-    peers += [partner, along_x(1), along_x(XS - 1)]
+    peers = [along_y(1), along_y(RING - 1), along_z(1), along_z(RING - 1), along_x(1), along_x(XS - 1), partner]
     for peer in peers:
         pl.semaphore_signal(barrier, inc=1, device_id=peer, device_id_type=MESH)
+
+    loads = []
+
+    def load(src, dst):
+        copy = pltpu.make_async_copy(src, dst, fetch.at[len(loads)])
+        copy.start()
+        loads.append(copy)
+        return copy
+
+    tables = [load(feat_in.at[pl.ds(c * LANES, LANES)], feat.at[pl.ds(c * LANES, LANES)]) for c in range(CHUNKS)]
+    small = [load(codes_in, codes_v), load(counts_in, counts), load(req_in, req_v), load(hub_in, hub_id)]
+    large = [load(own_in, own), load(weight_in, weight), load(bias_in, bias)]
 
     def push(src, dst, send, recv, peer):
         return pltpu.make_async_remote_copy(
             src_ref=src, dst_ref=dst, send_sem=send, recv_sem=recv, device_id=peer, device_id_type=MESH
         )
 
-    for half in range(2):
-        for chunk in range(CHUNKS):
-            block = feat[chunk * LANES : (chunk + 1) * LANES, half * LANES : (half + 1) * LANES]
-            ag[half, 0, chunk] = jnp.transpose(block)
-
-    codes = codes_t[...]
-    owner = (codes - HUBS) >> 5
-    slot = (codes - HUBS) & 31
-
-    def look(d, found):
-        return jnp.where(owner == d, counts[d], found)
-
-    filled = lax.fori_loop(0, RING * RING, look, jnp.zeros_like(codes), unroll=8)
-    live = (codes >= 0) & ((codes < HUBS) | (slot < filled))
-    codes = jnp.where(live, codes, -1)
-    taken[...] = 1.0 + jnp.sum(live.astype(jnp.float32), axis=0, keepdims=True)
-    for half, source in enumerate((req, req_t)):
-        turned = pltpu.roll(source[...], (spot[half] % 4) * CAP, 1)
-        for place in range(RING):
-            meta_tx[half, place, 0:16] = codes
-            meta_tx[half, place, 16:24] = turned[place * RING : (place + 1) * RING]
-        meta_rx[half, spot[half], 0:16] = codes
-    for half in range(2):
-        meta_rx[half, spot[half], 16:24] = meta_tx[half, spot[half], 16:24]
-
-    hub_sum = jnp.zeros((4 * LANES, LANES), jnp.float32)
-    for chunk in range(CHUNKS):
-        block = jnp.concatenate([ag[0, 0, chunk], ag[1, 0, chunk]], axis=0)
-        rows = lax.broadcasted_iota(jnp.int32, (LANES, LANES), 0) + chunk * LANES
-        pick = jnp.where(rows == hub_id[...], 1.0, 0.0).astype(jnp.bfloat16)
-        hub_sum = hub_sum + dot(split(block), pick)
-    hubs[0] = hub_sum[: 2 * LANES] + hub_sum[2 * LANES :]
-
-    pl.semaphore_wait(barrier, len(peers))
-
     sent = []
 
     def launch(copy):
         copy.start()
         sent.append(copy)
-
-    metas = []
-    for step in (4, 3, 5, 2, 6, 1, 7):
-        for half in range(2):
-            place = (spot[half] + step) % RING
-            copy = push(
-                meta_tx.at[half, place], meta_rx.at[half, spot[half]],
-                meta_send.at[half, step - 1], meta_recv.at[half, step - 1], cross[half](step),
-            )
-            launch(copy)
-            metas.append(copy)
 
     def table(half, way, wave, chunk):
         slot_from = wave if way == 0 else (RING - wave) % RING
@@ -126,11 +92,91 @@
         )
 
     moves = {}
-    for chunk in range(CHUNKS):
+
+    def turn(chunk):
+        tables[chunk].wait()
+        for half in range(2):
+            block = feat[chunk * LANES : (chunk + 1) * LANES, half * LANES : (half + 1) * LANES]
+            ag[half, 0, chunk] = jnp.transpose(block)
+
+    def send_own(chunk):
         for half in range(2):
             for way in range(2):
                 moves[half, way, 0, chunk] = table(half, way, 0, chunk)
                 launch(moves[half, way, 0, chunk])
+
+    def tell(half, way):
+        peer = ring[half](1 if way == 0 else RING - 1)
+        pl.semaphore_signal(token.at[half, way], inc=1, device_id=peer, device_id_type=MESH)
+
+    cblk[...] = jnp.zeros_like(cblk)
+    pacc[...] = jnp.zeros_like(pacc)
+    turn(0)
+    pl.semaphore_wait(barrier, len(peers))
+    for half in range(2):
+        for way in range(2):
+            tell(half, way)
+    send_own(0)
+    turn(1)
+    send_own(1)
+
+    for copy in small:
+        copy.wait()
+    codes = jnp.concatenate([codes_v[...], jnp.full((1, LANES), -1, jnp.int32)], axis=0)
+    owner = (codes - HUBS) >> 5
+    slot = (codes - HUBS) & 31
+
+    def look(d, found):
+        return jnp.where(owner == d, counts[d], found)
+
+    filled = lax.fori_loop(0, RING * RING, look, jnp.zeros_like(codes), unroll=8)
+    live = (codes >= 0) & ((codes < HUBS) | (slot < filled))
+    codes = jnp.where(live, codes, -1)
+    taken[...] = 1.0 + jnp.sum(live.astype(jnp.float32), axis=0, keepdims=True)
+    req[...] = jnp.transpose(req_v[...])
+    lane = lax.broadcasted_iota(jnp.int32, (RING, LANES), 1) // CAP
+    for half in range(2):
+        for place in range(RING):
+            if half == 0:
+                lists = req[place * RING : (place + 1) * RING]
+            else:
+                lists = req[pl.ds(place, RING, stride=RING)]
+            lists = jnp.concatenate([lists] * 4, axis=1)
+            meta_tx[half, place, 0:16] = codes
+            meta_tx[half, place, 16:24] = jnp.where(lane == spot[half] % 4, lists, 0)
+        meta_rx[half, spot[half], 0:16] = codes
+    for half in range(2):
+        meta_rx[half, spot[half], 16:24] = meta_tx[half, spot[half], 16:24]
+
+    for hop in range(3):
+        for way in range(2):
+            for half in range(2):
+                if hop < 2 or way == 0:
+                    pl.semaphore_wait(token.at[half, way], 1)
+                    if hop + way < 2:
+                        tell(half, way)
+
+    metas = []
+    for step in (4, 3, 5, 2, 6, 1, 7):
+        for half in range(2):
+            place = (spot[half] + step) % RING
+            copy = push(
+                meta_tx.at[half, place], meta_rx.at[half, spot[half]],
+                meta_send.at[half, step - 1], meta_recv.at[half, step - 1], cross[half](step),
+            )
+            launch(copy)
+            metas.append(copy)
+    for chunk in range(2, CHUNKS):
+        turn(chunk)
+        send_own(chunk)
+
+    hub_sum = jnp.zeros((4 * LANES, LANES), jnp.float32)
+    for chunk in range(CHUNKS):
+        block = jnp.concatenate([ag[0, 0, chunk], ag[1, 0, chunk]], axis=0)
+        rows = lax.broadcasted_iota(jnp.int32, (LANES, LANES), 0) + chunk * LANES
+        pick = jnp.where(rows == hub_id[...], 1.0, 0.0).astype(jnp.bfloat16)
+        hub_sum = hub_sum + dot(split(block), pick)
+    hubs[0] = hub_sum[: 2 * LANES] + hub_sum[2 * LANES :]
 
     def hub_push(index, src, dst, peer):
         copy = push(src, dst, hub_send.at[index], hub_recv.at[index], peer)
@@ -141,10 +187,20 @@
     hub_left = hub_push(1, hubs.at[0], hubs.at[6], along_x(XS - 1))
     hub_over = [hub_push(2, hubs.at[0], hubs.at[1], partner)]
 
-    cblk[...] = jnp.zeros_like(cblk)
-    pacc[...] = jnp.zeros_like(pacc)
+    for copy in large:
+        copy.wait()
     tot[...] = jnp.transpose(own[...])
 
+    def relay(wave, chunk):
+        for half in range(2):
+            for way in range(2):
+                moves[half, way, wave - 1, chunk].wait_recv()
+                if wave < 3 or chunk // 2 == way:
+                    moves[half, way, wave, chunk] = table(half, way, wave, chunk)
+                    launch(moves[half, way, wave, chunk])
+
+    relay(1, 0)
+    relay(1, 1)
     for copy in metas:
         copy.wait_recv()
     for half in range(2):
@@ -213,12 +269,8 @@
 
     for wave in range(1, 4):
         for chunk in range(CHUNKS):
-            for half in range(2):
-                for way in range(2):
-                    moves[half, way, wave - 1, chunk].wait_recv()
-                    if wave < 3 or chunk // 2 == way:
-                        moves[half, way, wave, chunk] = table(half, way, wave, chunk)
-                        launch(moves[half, way, wave, chunk])
+            if wave > 1 or chunk > 1:
+                relay(wave, chunk)
             if chunk == 1:
                 lax.fori_loop(0, 4, functools.partial(first_part, wave), 0)
             if chunk == 3:
@@ -273,18 +325,25 @@
 
 
 def local(features, seed_self, hub_ids, requests, counts, neighbors, weight, out_bias):
-    codes_t = jnp.pad(neighbors.T, ((0, 16 - FAN), (0, 0)), constant_values=-1)
-    req = jnp.pad(requests, ((0, 0), (0, LANES - CAP)))
-    req_t = req.reshape(RING, RING, LANES).transpose(1, 0, 2).reshape(RING * RING, LANES)
+    hbm = pl.BlockSpec(memory_space=pltpu.HBM)
     vmem = pl.BlockSpec(memory_space=pltpu.VMEM)
-    smem = pl.BlockSpec(memory_space=pltpu.SMEM)
     dma = pltpu.SemaphoreType.DMA
     return pl.pallas_call(
         kernel,
         out_shape=jax.ShapeDtypeStruct((SEEDS, 2 * LANES), jnp.float32),
-        in_specs=[vmem] * 5 + [smem] + [vmem] * 3,
+        in_specs=[hbm] * 8,
         out_specs=vmem,
         scratch_shapes=[
+            pltpu.VMEM((ROWS, 2 * LANES), jnp.float32),
+            pltpu.VMEM((SEEDS, 2 * LANES), jnp.float32),
+            pltpu.VMEM((1, LANES), jnp.int32),
+            pltpu.VMEM((CAP, RING * RING), jnp.int32),
+            pltpu.VMEM((RING * RING, CAP), jnp.int32),
+            pltpu.SMEM((RING * RING,), jnp.int32),
+            pltpu.VMEM((FAN, SEEDS), jnp.int32),
+            pltpu.VMEM((2 * LANES, 2 * LANES), jnp.float32),
+            pltpu.VMEM((1, 2 * LANES), jnp.float32),
+            dma((11,)),
             pltpu.VMEM((2, RING, CHUNKS, LANES, LANES), jnp.float32),
             pltpu.VMEM((2, RING, 24, LANES), jnp.int32),
             pltpu.VMEM((2, RING, 24, LANES), jnp.int32),
@@ -304,10 +363,11 @@
             dma((2, RING - 1)),
             dma((8,)),
             dma((8,)),
+            pltpu.SemaphoreType.REGULAR((2, 2)),
         ],
-        compiler_params=pltpu.CompilerParams(collective_id=0, has_side_effects=True, vmem_limit_bytes=48 * 1024 * 1024),
+        compiler_params=pltpu.CompilerParams(collective_id=0, has_side_effects=True),
         name="sage",
-    )(features, seed_self, hub_ids.reshape(1, LANES), req, req_t, counts, codes_t, weight, out_bias.reshape(1, 2 * LANES))
+    )(features, seed_self, hub_ids.reshape(1, LANES), requests.T, counts, neighbors.T, weight, out_bias.reshape(1, 2 * LANES))
 
 
 def solution(mesh):

time: 60.6 us -> 57.8 us (0.954)
  the two profiles are of different devices: /device:TPU:6 before, /device:TPU:1 now
where the time goes in v2:
time: 57.8 us; the launch traced here: 57.6 us
  Pallas kernels  56.1 us (97%)
  local copies, waits for them, and re-layouts  1.57 us (3%)
    pallas_call x1, Pallas kernels, local(): pl.pallas_call(kernel, out_shape=jax.ShapeDtypeStruct((SEEDS, 2 * LANES),...  56.1 us
    unnamed x1, local copies, waits for them, and re-layouts  1.57 us

profile of v2, /device:TPU:1, one launch (start us, length us, event | category | flops | bytes accessed | tf_op | source)
XLA Modules:
  0.0 57.6 jit_solution(16116659623097758679)
XLA Ops:
  0.0 56.1 %sage.1 = f32[128,256]{1,0:T(8,128)} custom-call(f32[512,256]{1,0:T(8,128)} %feat_in.1, f32[128,256]{1,0:T(8,128)} %own_in.1, s32[1,128]{1,0:T(1,128)} %bitcast.7, s32[32,64]{1,0:T(8,128)} %bitcast.4, s32[64]{0:T(128)} %counts_in.1, s32[15,128]{1,0:T(8,128)} %bitcast.5, f32[256,256]{1,0:T(8,128)} %weight_in.1, f32[1,256]{1,0:T(1,128)} %bitcast.6), custom_call_target="tpu_custom_call" | custom-call | tf_op jit(solution)/shard_map/sage/pallas_call | solution.py:331
  56.1 1.6 %copy.10 = f32[128,256]{1,0:T(8,128)} copy(f32[128,256]{1,0:T(8,128)} %sage.1) | data formatting | bytes 262144

commit v3 on v2

v3 whole, which is shorter than its diff:
```python
import functools

import jax
import jax.numpy as jnp
from jax import lax
from jax.experimental import pallas as pl
from jax.experimental.pallas import tpu as pltpu
from jax.sharding import PartitionSpec as P

MESH = pl.DeviceIdType.MESH
RING = 8
XS = 4
ROWS = 512
SEEDS = 128
FAN = 15
CAP = 32
HUBS = 1024
CHUNKS = 4
LANES = 128
WIDE = 64


def split(values):
    high = values.astype(jnp.bfloat16)
    low = (values - high.astype(jnp.float32)).astype(jnp.bfloat16)
    return jnp.concatenate([high, low], axis=0)


def dot(left, right):
    return jnp.dot(left, right, preferred_element_type=jnp.float32)


def kernel(
    feat_in, own_in, hub_in, req_in, counts_in, codes_in, weight_in, bias_in, out,
    feat, own, hub_id, req_v, req, counts, codes_v, weight, bias, fetch,
    ag, meta_tx, meta_rx, ids, cblk, pacc, part, hubs, tot, taken,
    ag_send, ag_recv, meta_send, meta_recv, part_send, part_recv, hub_send, hub_recv, token,
):
    rep = lax.axis_index("rep")
    shard = lax.axis_index("shard")
    me_x, core = rep // 2, rep % 2
    me = (shard % RING, shard // RING)

    def along_y(step):
        return {"rep": rep, "shard": me[1] * RING + (me[0] + step) % RING}

    def along_z(step):
        return {"rep": rep, "shard": ((me[1] + step) % RING) * RING + me[0]}

    def along_x(step):
        return {"rep": ((me_x + step) % XS) * 2 + core, "shard": shard}

    ring = (along_y, along_z)
    cross = (along_z, along_y)
    spot = (me[1], me[0])

    barrier = pltpu.get_barrier_semaphore()
    partner = {"rep": me_x * 2 + 1 - core, "shard": shard}
    peers = [along_y(1), along_y(RING - 1), along_z(1), along_z(RING - 1), along_x(1), along_x(XS - 1), partner]
    for peer in peers:
        pl.semaphore_signal(barrier, inc=1, device_id=peer, device_id_type=MESH)

    loads = []

    def load(src, dst):
        copy = pltpu.make_async_copy(src, dst, fetch.at[len(loads)])
        copy.start()
        loads.append(copy)
        return copy

    tables = [load(feat_in.at[pl.ds(c * LANES, LANES)], feat.at[pl.ds(c * LANES, LANES)]) for c in range(CHUNKS)]
    small = [load(codes_in, codes_v), load(counts_in, counts), load(req_in, req_v), load(hub_in, hub_id)]
    large = [load(own_in, own), load(weight_in, weight), load(bias_in, bias)]

    def push(src, dst, send, recv, peer):
        return pltpu.make_async_remote_copy(
            src_ref=src, dst_ref=dst, send_sem=send, recv_sem=recv, device_id=peer, device_id_type=MESH
        )

    sent = []

    def launch(copy):
        copy.start()
        sent.append(copy)
        return copy

    def table(half, way, wave, group, turn):
        piece = turn if way == 0 else 1 - turn
        slot_from = wave if way == 0 else (RING - wave) % RING
        slot_to = wave + 1 if way == 0 else RING - wave - 1
        return push(
            ag.at[half, slot_from, group, piece], ag.at[half, slot_to, group, piece],
            ag_send.at[half, way, wave, group, turn], ag_recv.at[half, slot_to, group, piece],
            ring[half](1 if way == 0 else RING - 1),
        )

    moves = {}

    def send_own(group):
        for turn in range(2):
            for half in range(2):
                for way in range(2):
                    moves[half, way, 0, group, turn] = launch(table(half, way, 0, group, turn))

    def tell(half, way):
        peer = ring[half](1 if way == 0 else RING - 1)
        pl.semaphore_signal(token.at[half, way], inc=1, device_id=peer, device_id_type=MESH)

    cblk[...] = jnp.zeros_like(cblk)
    for chunk in range(CHUNKS):
        tables[chunk].wait()
        for half in range(2):
            block = jnp.transpose(feat[chunk * LANES : (chunk + 1) * LANES, half * LANES : (half + 1) * LANES])
            left = (chunk % 2) * LANES
            for group in range(2):
                ag[half, 0, group, chunk // 2, :, left : left + LANES] = block[group * WIDE : (group + 1) * WIDE]
    pl.semaphore_wait(barrier, len(peers))
    for half in range(2):
        for way in range(2):
            tell(half, way)
    send_own(0)

    for copy in small:
        copy.wait()
    codes = jnp.concatenate([codes_v[...], jnp.full((1, LANES), -1, jnp.int32)], axis=0)
    owner = (codes - HUBS) >> 5
    slot = (codes - HUBS) & 31

    def look(d, found):
        return jnp.where(owner == d, counts[d], found)

    filled = lax.fori_loop(0, RING * RING, look, jnp.zeros_like(codes), unroll=8)
    live = (codes >= 0) & ((codes < HUBS) | (slot < filled))
    codes = jnp.where(live, codes, -1)
    taken[...] = 1.0 + jnp.sum(live.astype(jnp.float32), axis=0, keepdims=True)
    req[...] = jnp.transpose(req_v[...])
    lane = lax.broadcasted_iota(jnp.int32, (RING, LANES), 1) // CAP
    for half in range(2):
        for place in range(RING):
            if half == 0:
                lists = req[place * RING : (place + 1) * RING]
            else:
                lists = req[pl.ds(place, RING, stride=RING)]
            lists = jnp.concatenate([lists] * 4, axis=1)
            meta_tx[half, place, 0:16] = codes
            meta_tx[half, place, 16:24] = jnp.where(lane == spot[half] % 4, lists, 0)
        meta_rx[half, spot[half], 0:16] = codes
    for half in range(2):
        meta_rx[half, spot[half], 16:24] = meta_tx[half, spot[half], 16:24]

    for hop in range(3):
        for way in range(2):
            for half in range(2):
                if hop < 2 or way == 0:
                    pl.semaphore_wait(token.at[half, way], 1)
                    if hop + way < 2:
                        tell(half, way)

    metas = []
    for step in (4, 3, 5, 2, 6, 1, 7):
        for half in range(2):
            place = (spot[half] + step) % RING
            copy = push(
                meta_tx.at[half, place], meta_rx.at[half, spot[half]],
                meta_send.at[half, step - 1], meta_recv.at[half, step - 1], cross[half](step),
            )
            launch(copy)
            metas.append(copy)
    send_own(1)

    hub_sum = jnp.zeros((4 * LANES, LANES), jnp.float32)
    for piece in range(2):
        block = jnp.concatenate([ag[half, 0, group, piece] for half in range(2) for group in range(2)], axis=0)
        rows = lax.broadcasted_iota(jnp.int32, (2 * LANES, LANES), 0) + piece * 2 * LANES
        pick = jnp.where(rows == hub_id[...], 1.0, 0.0).astype(jnp.bfloat16)
        hub_sum = hub_sum + dot(split(block), pick)
    hubs[0] = hub_sum[: 2 * LANES] + hub_sum[2 * LANES :]

    def hub_push(index, src, dst, peer):
        copy = push(src, dst, hub_send.at[index], hub_recv.at[index], peer)
        launch(copy)
        return copy

    hub_right = hub_push(0, hubs.at[0], hubs.at[2], along_x(1))
    hub_left = hub_push(1, hubs.at[0], hubs.at[6], along_x(XS - 1))
    hub_over = [hub_push(2, hubs.at[0], hubs.at[1], partner)]

    for copy in large:
        copy.wait()
    tot[...] = jnp.transpose(own[...])

    def relay(wave, group, turn):
        for half in range(2):
            for way in range(2):
                moves[half, way, wave - 1, group, turn].wait_recv()
                if wave < 3 or turn == 0:
                    moves[half, way, wave, group, turn] = launch(table(half, way, wave, group, turn))

    def place_of(half, slot_index):
        return (me[half] + RING - slot_index) % RING

    def lay_counts(slots):
        for half in range(2):
            for slot_index in slots:
                origin = place_of(half, slot_index)
                number = me[1] * RING + origin if half == 0 else origin * RING + me[0]
                lines = lax.broadcasted_iota(jnp.int32, (CAP, LANES), 0) + (HUBS + number * CAP)
                for place in range(RING):
                    count = jnp.zeros((CAP, LANES), jnp.float32)
                    for k in range(FAN):
                        count = count + jnp.where(meta_rx[half, place, k : k + 1] == lines, 1.0, 0.0)
                    top, left = CAP * (place % 4), LANES * (place % 2)
                    cblk[half, slot_index, place // 2, top : top + CAP, left : left + LANES] = count.astype(jnp.bfloat16)

    def add_block(half, slot_index, group):
        block = jnp.concatenate([ag[half, slot_index, group, piece] for piece in range(2)], axis=1)
        wanted = ids[half, pl.ds(place_of(half, slot_index), 1), :]
        rows = lax.broadcasted_iota(jnp.int32, (ROWS, 2 * LANES), 0)
        found = dot(split(block), jnp.where(rows == wanted, 1.0, 0.0).astype(jnp.bfloat16)).astype(jnp.bfloat16)
        for pair in range(RING // 2):
            side = (pair // 2) * LANES
            sums = dot(found[:, side : side + LANES], cblk[half, slot_index, pair])
            sums = sums[:WIDE] + sums[WIDE:]
            for k in range(2):
                piece = sums[:, k * LANES : (k + 1) * LANES]
                if slot_index == 0:
                    pacc[half, 2 * pair + k, group] = piece
                else:
                    pacc[half, 2 * pair + k, group] += piece

    def add_blocks(slots, group):
        for slot_index in slots:
            for half in range(2):
                add_block(half, slot_index, group)

    def hub_block(index, carry):
        chip, over = index // 2, index % 2
        origin = ((me_x + XS - chip) % XS) * 2 + (core + over) % 2
        lines = lax.broadcasted_iota(jnp.int32, (LANES, LANES), 0) + origin * LANES
        mine = spot[0]
        count = jnp.zeros((LANES, LANES), jnp.float32)
        for k in range(FAN):
            count = count + jnp.where(meta_rx[0, mine, k : k + 1] == lines, 1.0, 0.0)
        sums = dot(split(hubs[index]), count.astype(jnp.bfloat16))
        tot[...] += sums[: 2 * LANES] + sums[2 * LANES :]
        return carry

    relay(1, 0, 0)
    relay(1, 0, 1)
    for copy in metas:
        copy.wait_recv()
    for half in range(2):
        for group in range(2):
            tiles = [meta_rx[half, 4 * group + k, 16:24] for k in range(4)]
            ids[half, :, group * LANES : (group + 1) * LANES] = tiles[0] + tiles[1] + tiles[2] + tiles[3]
    lay_counts((0,))
    add_blocks((0,), 0)
    add_blocks((0,), 1)
    relay(1, 1, 0)
    relay(1, 1, 1)
    hub_right.wait_recv()
    hub_left.wait_recv()
    low, high = pl.ds(0, LANES), pl.ds(LANES, LANES)
    far = [
        hub_push(3, hubs.at[2, low], hubs.at[4, low], along_x(1)),
        hub_push(4, hubs.at[6, high], hubs.at[4, high], along_x(XS - 1)),
    ]
    hub_over.append(hub_push(5, hubs.at[2], hubs.at[3], partner))
    hub_over.append(hub_push(6, hubs.at[6], hubs.at[7], partner))
    lay_counts((1, 7))
    add_blocks((1, 7), 0)
    relay(2, 0, 0)
    relay(2, 0, 1)
    for copy in far:
        copy.wait_recv()
    hub_over.append(hub_push(7, hubs.at[4], hubs.at[5], partner))
    add_blocks((1, 7), 1)
    lay_counts((2, 6))
    relay(2, 1, 0)
    add_blocks((2, 6), 0)
    relay(3, 0, 0)
    lay_counts((3, 5))
    relay(2, 1, 1)
    relay(3, 0, 1)
    add_blocks((3, 5), 0)
    lay_counts((4,))
    relay(3, 1, 0)
    add_blocks((2, 6), 1)

    sums_moves = []

    def finish(group):
        for half in range(2):
            for way in range(2):
                moves[half, way, 3, group, 0].wait_recv()
        for half in range(2):
            add_block(half, 4, group)
            for step in (4, 3, 5, 2, 6, 1, 7):
                copy = push(
                    pacc.at[half, (spot[half] + step) % RING, group], part.at[half, step - 1, group],
                    part_send.at[half, group, step - 1], part_recv.at[half, group, step - 1], cross[half](step),
                )
                launch(copy)
                sums_moves.append((half, step, group, copy))

    finish(0)
    relay(3, 1, 1)
    add_blocks((3, 5), 1)
    finish(1)
    for copy in hub_over:
        copy.wait_recv()
    lax.fori_loop(0, 8, hub_block, 0, unroll=True)

    product = jnp.zeros((SEEDS, 2 * LANES), jnp.float32)
    for group in range(2):
        lines = []
        for half in range(2):
            top = half * LANES + group * WIDE
            total = tot[top : top + WIDE] + pacc[half, spot[half], group]
            for wanted in (1, 7, 2, 6, 3, 5, 4):
                for side, step, number, copy in sums_moves:
                    if (side, step, number) == (half, wanted, group):
                        copy.wait_recv()
                        total = total + part[half, step - 1, group]
            lines.append(total)
        mean = jnp.transpose(jnp.concatenate(lines, axis=0) / taken[...])
        parts = [weight[half * LANES + group * WIDE : half * LANES + (group + 1) * WIDE] for half in range(2)]
        product = product + jnp.dot(
            mean, jnp.concatenate(parts, axis=0), precision=lax.Precision.HIGHEST, preferred_element_type=jnp.float32
        )
    out[...] = jnp.maximum(product + bias[...], 0.0)
    for copy in sent:
        copy.wait_send()


def local(features, seed_self, hub_ids, requests, counts, neighbors, weight, out_bias):
    hbm = pl.BlockSpec(memory_space=pltpu.HBM)
    vmem = pl.BlockSpec(memory_space=pltpu.VMEM)
    dma = pltpu.SemaphoreType.DMA
    return pl.pallas_call(
        kernel,
        out_shape=jax.ShapeDtypeStruct((SEEDS, 2 * LANES), jnp.float32),
        in_specs=[hbm] * 8,
        out_specs=vmem,
        scratch_shapes=[
            pltpu.VMEM((ROWS, 2 * LANES), jnp.float32),
            pltpu.VMEM((SEEDS, 2 * LANES), jnp.float32),
            pltpu.VMEM((1, LANES), jnp.int32),
            pltpu.VMEM((CAP, RING * RING), jnp.int32),
            pltpu.VMEM((RING * RING, CAP), jnp.int32),
            pltpu.SMEM((RING * RING,), jnp.int32),
            pltpu.VMEM((FAN, SEEDS), jnp.int32),
            pltpu.VMEM((2 * LANES, 2 * LANES), jnp.float32),
            pltpu.VMEM((1, 2 * LANES), jnp.float32),
            dma((11,)),
            pltpu.VMEM((2, RING, 2, 2, WIDE, 2 * LANES), jnp.float32),
            pltpu.VMEM((2, RING, 24, LANES), jnp.int32),
            pltpu.VMEM((2, RING, 24, LANES), jnp.int32),
            pltpu.VMEM((2, RING, 2 * LANES), jnp.int32),
            pltpu.VMEM((2, RING, 4, LANES, 2 * LANES), jnp.bfloat16),
            pltpu.VMEM((2, RING, 2, WIDE, LANES), jnp.float32),
            pltpu.VMEM((2, RING - 1, 2, WIDE, LANES), jnp.float32),
            pltpu.VMEM((2 * XS, 2 * LANES, LANES), jnp.float32),
            pltpu.VMEM((2 * LANES, LANES), jnp.float32),
            pltpu.VMEM((1, LANES), jnp.float32),
            dma((2, 2, 4, 2, 2)),
            dma((2, RING, 2, 2)),
            dma((2, RING - 1)),
            dma((2, RING - 1)),
            dma((2, 2, RING - 1)),
            dma((2, 2, RING - 1)),
            dma((8,)),
            dma((8,)),
            pltpu.SemaphoreType.REGULAR((2, 2)),
        ],
        compiler_params=pltpu.CompilerParams(collective_id=0, has_side_effects=True),
        name="sage",
    )(features, seed_self, hub_ids.reshape(1, LANES), requests.T, counts, neighbors.T, weight, out_bias.reshape(1, 2 * LANES))


def solution(mesh):
    rows, flat = P(("rep", "shard"), None), P(("rep", "shard"))
    return jax.shard_map(
        local, mesh=mesh, in_specs=(rows, rows, flat, rows, flat, rows, P(), P()), out_specs=rows, check_vma=False
    )
```

time: 57.8 us -> 54.2 us (0.938)
  the two profiles are of different devices: /device:TPU:1 before, /device:TPU:4 now
where the time goes in v3:
time: 54.2 us; the launch traced here: 54 us
  Pallas kernels  52.4 us (97%)
  local copies, waits for them, and re-layouts  1.57 us (3%)
    pallas_call x1, Pallas kernels, local(): pl.pallas_call(kernel, out_shape=jax.ShapeDtypeStruct((SEEDS, 2 * LANES),...  52.4 us
    unnamed x1, local copies, waits for them, and re-layouts  1.57 us

profile of v3, /device:TPU:4, one launch (start us, length us, event | category | flops | bytes accessed | tf_op | source)
XLA Modules:
  0.0 54.0 jit_solution(8077256817491720011)
XLA Ops:
  0.0 52.4 %sage.1 = f32[128,256]{1,0:T(8,128)} custom-call(f32[512,256]{1,0:T(8,128)} %feat_in.1, f32[128,256]{1,0:T(8,128)} %own_in.1, s32[1,128]{1,0:T(1,128)} %bitcast.7, s32[32,64]{1,0:T(8,128)} %bitcast.4, s32[64]{0:T(128)} %counts_in.1, s32[15,128]{1,0:T(8,128)} %bitcast.5, f32[256,256]{1,0:T(8,128)} %weight_in.1, f32[1,256]{1,0:T(1,128)} %bitcast.6), custom_call_target="tpu_custom_call" | custom-call | tf_op jit(solution)/shard_map/sage/pallas_call | solution.py:340
  52.4 1.6 %copy.10 = f32[128,256]{1,0:T(8,128)} copy(f32[128,256]{1,0:T(8,128)} %sage.1) | data formatting | bytes 262144

commit v4 on v3

--- a/solution.py
+++ b/solution.py
@@ -373,9 +373,17 @@
             dma((8,)),
             pltpu.SemaphoreType.REGULAR((2, 2)),
         ],
-        compiler_params=pltpu.CompilerParams(collective_id=0, has_side_effects=True),
+        compiler_params=pltpu.CompilerParams(collective_id=0, has_side_effects=True, vmem_limit_bytes=40 * 1024 * 1024),
         name="sage",
-    )(features, seed_self, hub_ids.reshape(1, LANES), requests.T, counts, neighbors.T, weight, out_bias.reshape(1, 2 * LANES))
+    )(
+        *(
+            pltpu.with_memory_space_constraint(x, pltpu.HBM)
+            for x in (
+                features, seed_self, hub_ids.reshape(1, LANES), requests.T, counts, neighbors.T, weight,
+                out_bias.reshape(1, 2 * LANES),
+            )
+        )
+    )
 
 
 def solution(mesh):

time: 54.2 us -> 52.6 us (0.970)
  local copies, waits for them, and re-layouts: 1.57 us -> 0.66 us
  Pallas kernels: 52.4 us -> 51.8 us
    unnamed x1, local copies, waits for them, and re-layouts: 1.57 us -> 0.66 us
    pallas_call x1, Pallas kernels: 52.4 us -> 51.8 us  [local(): pl.pallas_call(kernel, out_shape=jax.ShapeDtypeStruct((SEEDS, 2 * LANES),...]
where the time goes in v4:
time: 52.6 us; the launch traced here: 52.5 us
  Pallas kernels  51.8 us (98%)
  local copies, waits for them, and re-layouts  0.66 us (1%)
    pallas_call x1, Pallas kernels, local(): pl.pallas_call(kernel, out_shape=jax.ShapeDtypeStruct((SEEDS, 2 * LANES),...  51.8 us

profile of v4, /device:TPU:4, one launch (start us, length us, event | category | flops | bytes accessed | tf_op | source)
XLA Modules:
  0.0 52.5 jit_solution(11565436057644773440)
XLA Ops:
  0.0 51.8 %sage.1 = f32[128,256]{1,0:T(8,128)S(1)} custom-call(f32[512,256]{1,0:T(8,128)} %feat_in.1, f32[128,256]{1,0:T(8,128)} %own_in.1, s32[1,128]{1,0:T(1,128)} %bitcast.7, s32[32,64]{1,0:T(8,128)} %bitcast.4, s32[64]{0:T(128)} %counts_in.1, s32[15,128]{1,0:T(8,128)} %bitcast.5, f32[256,256]{1,0:T(8,128)} %weight_in.1, f32[1,256]{1,0:T(1,128)} %bitcast.6), custom_call_target="tpu_custom_call" | custom-call | tf_op jit(solution)/shard_map/sage/pallas_call | solution.py:340
  51.8 0.7 %copy.10 = f32[128,256]{1,0:T(8,128)} copy(f32[128,256]{1,0:T(8,128)S(1)} %sage.1) | data formatting | bytes 262144

commit v5 on v4

--- a/solution.py
+++ b/solution.py
@@ -34,7 +34,7 @@
     feat_in, own_in, hub_in, req_in, counts_in, codes_in, weight_in, bias_in, out,
     feat, own, hub_id, req_v, req, counts, codes_v, weight, bias, fetch,
     ag, meta_tx, meta_rx, ids, cblk, pacc, part, hubs, tot, taken,
-    ag_send, ag_recv, meta_send, meta_recv, part_send, part_recv, hub_send, hub_recv, token,
+    send, recv, ag_recv, token,
 ):
     rep = lax.axis_index("rep")
     shard = lax.axis_index("shard")
@@ -68,7 +68,7 @@
         loads.append(copy)
         return copy
 
-    tables = [load(feat_in.at[pl.ds(c * LANES, LANES)], feat.at[pl.ds(c * LANES, LANES)]) for c in range(CHUNKS)]
+    tables = load(feat_in, feat)
     small = [load(codes_in, codes_v), load(counts_in, counts), load(req_in, req_v), load(hub_in, hub_id)]
     large = [load(own_in, own), load(weight_in, weight), load(bias_in, bias)]
 
@@ -77,12 +77,12 @@
             src_ref=src, dst_ref=dst, send_sem=send, recv_sem=recv, device_id=peer, device_id_type=MESH
         )
 
-    sent = []
-
     def launch(copy):
         copy.start()
-        sent.append(copy)
         return copy
+
+    def drain(semaphore, view):
+        pltpu.make_async_copy(view, view, semaphore).wait()
 
     def table(half, way, wave, group, turn):
         piece = turn if way == 0 else 1 - turn
@@ -90,25 +90,23 @@
         slot_to = wave + 1 if way == 0 else RING - wave - 1
         return push(
             ag.at[half, slot_from, group, piece], ag.at[half, slot_to, group, piece],
-            ag_send.at[half, way, wave, group, turn], ag_recv.at[half, slot_to, group, piece],
+            send.at[0], ag_recv.at[half, wave, group, turn],
             ring[half](1 if way == 0 else RING - 1),
         )
-
-    moves = {}
 
     def send_own(group):
         for turn in range(2):
             for half in range(2):
                 for way in range(2):
-                    moves[half, way, 0, group, turn] = launch(table(half, way, 0, group, turn))
+                    launch(table(half, way, 0, group, turn))
 
     def tell(half, way):
         peer = ring[half](1 if way == 0 else RING - 1)
         pl.semaphore_signal(token.at[half, way], inc=1, device_id=peer, device_id_type=MESH)
 
     cblk[...] = jnp.zeros_like(cblk)
+    tables.wait()
     for chunk in range(CHUNKS):
-        tables[chunk].wait()
         for half in range(2):
             block = jnp.transpose(feat[chunk * LANES : (chunk + 1) * LANES, half * LANES : (half + 1) * LANES])
             left = (chunk % 2) * LANES
@@ -156,16 +154,14 @@
                     if hop + way < 2:
                         tell(half, way)
 
-    metas = []
     for step in (4, 3, 5, 2, 6, 1, 7):
         for half in range(2):
             place = (spot[half] + step) % RING
             copy = push(
                 meta_tx.at[half, place], meta_rx.at[half, spot[half]],
-                meta_send.at[half, step - 1], meta_recv.at[half, step - 1], cross[half](step),
+                send.at[1], recv.at[0], cross[half](step),
             )
             launch(copy)
-            metas.append(copy)
     send_own(1)
 
     hub_sum = jnp.zeros((4 * LANES, LANES), jnp.float32)
@@ -177,13 +173,11 @@
     hubs[0] = hub_sum[: 2 * LANES] + hub_sum[2 * LANES :]
 
     def hub_push(index, src, dst, peer):
-        copy = push(src, dst, hub_send.at[index], hub_recv.at[index], peer)
-        launch(copy)
-        return copy
-
-    hub_right = hub_push(0, hubs.at[0], hubs.at[2], along_x(1))
-    hub_left = hub_push(1, hubs.at[0], hubs.at[6], along_x(XS - 1))
-    hub_over = [hub_push(2, hubs.at[0], hubs.at[1], partner)]
+        launch(push(src, dst, send.at[2], recv.at[index], peer))
+
+    hub_push(1, hubs.at[0], hubs.at[2], along_x(1))
+    hub_push(1, hubs.at[0], hubs.at[6], along_x(XS - 1))
+    hub_push(3, hubs.at[0], hubs.at[1], partner)
 
     for copy in large:
         copy.wait()
@@ -191,10 +185,10 @@
 
     def relay(wave, group, turn):
         for half in range(2):
-            for way in range(2):
-                moves[half, way, wave - 1, group, turn].wait_recv()
-                if wave < 3 or turn == 0:
-                    moves[half, way, wave, group, turn] = launch(table(half, way, wave, group, turn))
+            drain(ag_recv.at[half, wave - 1, group, turn], ag.at[half, 0, 0])
+            if wave < 3 or turn == 0:
+                for way in range(2):
+                    launch(table(half, way, wave, group, turn))
 
     def place_of(half, slot_index):
         return (me[half] + RING - slot_index) % RING
@@ -247,8 +241,7 @@
 
     relay(1, 0, 0)
     relay(1, 0, 1)
-    for copy in metas:
-        copy.wait_recv()
+    drain(recv.at[0], meta_rx.at[:, pl.ds(0, RING - 1)])
     for half in range(2):
         for group in range(2):
             tiles = [meta_rx[half, 4 * group + k, 16:24] for k in range(4)]
@@ -258,22 +251,18 @@
     add_blocks((0,), 1)
     relay(1, 1, 0)
     relay(1, 1, 1)
-    hub_right.wait_recv()
-    hub_left.wait_recv()
+    drain(recv.at[1], hubs.at[pl.ds(0, 2)])
     low, high = pl.ds(0, LANES), pl.ds(LANES, LANES)
-    far = [
-        hub_push(3, hubs.at[2, low], hubs.at[4, low], along_x(1)),
-        hub_push(4, hubs.at[6, high], hubs.at[4, high], along_x(XS - 1)),
-    ]
-    hub_over.append(hub_push(5, hubs.at[2], hubs.at[3], partner))
-    hub_over.append(hub_push(6, hubs.at[6], hubs.at[7], partner))
+    hub_push(2, hubs.at[2, low], hubs.at[4, low], along_x(1))
+    hub_push(2, hubs.at[6, high], hubs.at[4, high], along_x(XS - 1))
+    hub_push(3, hubs.at[2], hubs.at[3], partner)
+    hub_push(3, hubs.at[6], hubs.at[7], partner)
     lay_counts((1, 7))
     add_blocks((1, 7), 0)
     relay(2, 0, 0)
     relay(2, 0, 1)
-    for copy in far:
-        copy.wait_recv()
-    hub_over.append(hub_push(7, hubs.at[4], hubs.at[5], partner))
+    drain(recv.at[2], hubs.at[0])
+    hub_push(3, hubs.at[4], hubs.at[5], partner)
     add_blocks((1, 7), 1)
     lay_counts((2, 6))
     relay(2, 1, 0)
@@ -287,41 +276,34 @@
     relay(3, 1, 0)
     add_blocks((2, 6), 1)
 
-    sums_moves = []
-
     def finish(group):
         for half in range(2):
-            for way in range(2):
-                moves[half, way, 3, group, 0].wait_recv()
-        for half in range(2):
+            drain(ag_recv.at[half, 3, group, 0], ag.at[half, 0, 0])
             add_block(half, 4, group)
             for step in (4, 3, 5, 2, 6, 1, 7):
-                copy = push(
-                    pacc.at[half, (spot[half] + step) % RING, group], part.at[half, step - 1, group],
-                    part_send.at[half, group, step - 1], part_recv.at[half, group, step - 1], cross[half](step),
+                launch(
+                    push(
+                        pacc.at[half, (spot[half] + step) % RING, group], part.at[group, half, step - 1],
+                        send.at[3], recv.at[4 + group], cross[half](step),
+                    )
                 )
-                launch(copy)
-                sums_moves.append((half, step, group, copy))
 
     finish(0)
     relay(3, 1, 1)
     add_blocks((3, 5), 1)
     finish(1)
-    for copy in hub_over:
-        copy.wait_recv()
+    drain(recv.at[3], hubs.at[pl.ds(0, 4)])
     lax.fori_loop(0, 8, hub_block, 0, unroll=True)
 
     product = jnp.zeros((SEEDS, 2 * LANES), jnp.float32)
     for group in range(2):
+        drain(recv.at[4 + group], part.at[group])
         lines = []
         for half in range(2):
             top = half * LANES + group * WIDE
             total = tot[top : top + WIDE] + pacc[half, spot[half], group]
-            for wanted in (1, 7, 2, 6, 3, 5, 4):
-                for side, step, number, copy in sums_moves:
-                    if (side, step, number) == (half, wanted, group):
-                        copy.wait_recv()
-                        total = total + part[half, step - 1, group]
+            for step in range(1, RING):
+                total = total + part[group, half, step - 1]
             lines.append(total)
         mean = jnp.transpose(jnp.concatenate(lines, axis=0) / taken[...])
         parts = [weight[half * LANES + group * WIDE : half * LANES + (group + 1) * WIDE] for half in range(2)]
@@ -329,8 +311,10 @@
             mean, jnp.concatenate(parts, axis=0), precision=lax.Precision.HIGHEST, preferred_element_type=jnp.float32
         )
     out[...] = jnp.maximum(product + bias[...], 0.0)
-    for copy in sent:
-        copy.wait_send()
+    drain(send.at[0], ag.at[:, pl.ds(0, RING - 1)])
+    drain(send.at[1], meta_tx.at[:, pl.ds(0, RING - 1)])
+    drain(send.at[2], hubs.at[pl.ds(0, 7)])
+    drain(send.at[3], part)
 
 
 def local(features, seed_self, hub_ids, requests, counts, neighbors, weight, out_bias):
@@ -352,25 +336,20 @@
             pltpu.VMEM((FAN, SEEDS), jnp.int32),
             pltpu.VMEM((2 * LANES, 2 * LANES), jnp.float32),
             pltpu.VMEM((1, 2 * LANES), jnp.float32),
-            dma((11,)),
+            dma((8,)),
             pltpu.VMEM((2, RING, 2, 2, WIDE, 2 * LANES), jnp.float32),
             pltpu.VMEM((2, RING, 24, LANES), jnp.int32),
             pltpu.VMEM((2, RING, 24, LANES), jnp.int32),
             pltpu.VMEM((2, RING, 2 * LANES), jnp.int32),
             pltpu.VMEM((2, RING, 4, LANES, 2 * LANES), jnp.bfloat16),
             pltpu.VMEM((2, RING, 2, WIDE, LANES), jnp.float32),
-            pltpu.VMEM((2, RING - 1, 2, WIDE, LANES), jnp.float32),
+            pltpu.VMEM((2, 2, RING - 1, WIDE, LANES), jnp.float32),
             pltpu.VMEM((2 * XS, 2 * LANES, LANES), jnp.float32),
             pltpu.VMEM((2 * LANES, LANES), jnp.float32),
             pltpu.VMEM((1, LANES), jnp.float32),
-            dma((2, 2, 4, 2, 2)),
-            dma((2, RING, 2, 2)),
-            dma((2, RING - 1)),
-            dma((2, RING - 1)),
-            dma((2, 2, RING - 1)),
-            dma((2, 2, RING - 1)),
-            dma((8,)),
-            dma((8,)),
+            dma((4,)),
+            dma((6,)),
+            dma((2, 4, 2, 2)),
             pltpu.SemaphoreType.REGULAR((2, 2)),
         ],
         compiler_params=pltpu.CompilerParams(collective_id=0, has_side_effects=True, vmem_limit_bytes=40 * 1024 * 1024),

time: 52.6 us -> 51.5 us (0.979)
  the two profiles are of different devices: /device:TPU:4 before, /device:TPU:6 now
where the time goes in v5:
time: 51.5 us; the launch traced here: 51.3 us
  Pallas kernels  50.7 us (98%)
  local copies, waits for them, and re-layouts  0.66 us (1%)
    pallas_call x1, Pallas kernels, local(): pl.pallas_call(kernel, out_shape=jax.ShapeDtypeStruct((SEEDS, 2 * LANES),...  50.7 us

profile of v5, /device:TPU:6, one launch (start us, length us, event | category | flops | bytes accessed | tf_op | source)
XLA Modules:
  0.0 51.3 jit_solution(9368594801760159322)
XLA Ops:
  0.0 50.7 %sage.1 = f32[128,256]{1,0:T(8,128)S(1)} custom-call(f32[512,256]{1,0:T(8,128)} %feat_in.1, f32[128,256]{1,0:T(8,128)} %own_in.1, s32[1,128]{1,0:T(1,128)} %bitcast.7, s32[32,64]{1,0:T(8,128)} %bitcast.4, s32[64]{0:T(128)} %counts_in.1, s32[15,128]{1,0:T(8,128)} %bitcast.5, f32[256,256]{1,0:T(8,128)} %weight_in.1, f32[1,256]{1,0:T(1,128)} %bitcast.6), custom_call_target="tpu_custom_call" | custom-call | tf_op jit(solution)/shard_map/sage/pallas_call | solution.py:324
  50.7 0.7 %copy.10 = f32[128,256]{1,0:T(8,128)} copy(f32[128,256]{1,0:T(8,128)S(1)} %sage.1) | data formatting | bytes 262144

commit v6 on v5

--- a/solution.py
+++ b/solution.py
@@ -33,8 +33,8 @@
 def kernel(
     feat_in, own_in, hub_in, req_in, counts_in, codes_in, weight_in, bias_in, out,
     feat, own, hub_id, req_v, req, counts, codes_v, weight, bias, fetch,
-    ag, meta_tx, meta_rx, ids, cblk, pacc, part, hubs, tot, taken,
-    send, recv, ag_recv, token,
+    ag, meta_tx, meta_rx, ids, cblk, pacc, part, far, mix, hubs, tot, taken,
+    send, recv, far_recv, ag_recv, token,
 ):
     rep = lax.axis_index("rep")
     shard = lax.axis_index("shard")
@@ -280,11 +280,42 @@
         for half in range(2):
             drain(ag_recv.at[half, 3, group, 0], ag.at[half, 0, 0])
             add_block(half, 4, group)
-            for step in (4, 3, 5, 2, 6, 1, 7):
+            here = spot[half]
+            for way in range(2):
+                sign = 1 - 2 * way
+                third = pacc.at[half, (here + 3 * sign + RING) % RING, group]
+                fourth = pacc.at[half, (here + 4) % RING, group, pl.ds(way * WIDE // 2, WIDE // 2)]
                 launch(
                     push(
-                        pacc.at[half, (spot[half] + step) % RING, group], part.at[group, half, step - 1],
-                        send.at[3], recv.at[4 + group], cross[half](step),
+                        fourth, far.at[group, half, way, pl.ds(WIDE, WIDE // 2)],
+                        send.at[3], far_recv.at[group, half], cross[half]((2 * sign) % RING),
+                    )
+                )
+                launch(
+                    push(
+                        third, far.at[group, half, way, pl.ds(0, WIDE)],
+                        send.at[3], far_recv.at[group, half], cross[half](sign % RING),
+                    )
+                )
+            for way in range(2):
+                sign = 1 - 2 * way
+                first = pacc.at[half, (here + sign + RING) % RING, group]
+                launch(push(first, part.at[group, half, way], send.at[4], recv.at[4 + group], cross[half](sign % RING)))
+
+    def combine(group):
+        for half in range(2):
+            drain(far_recv.at[group, half], far.at[group, half])
+            for way in range(2):
+                sign = 1 - 2 * way
+                rest = jnp.zeros((WIDE // 2, LANES), jnp.float32)
+                piece = far[group, half, way, WIDE:]
+                piece = jnp.concatenate([piece, rest] if way == 0 else [rest, piece], axis=0)
+                mine = pacc[half, (spot[half] + 2 * sign + RING) % RING, group]
+                mix[group, half, way] = mine + far[group, half, way, :WIDE] + piece
+                launch(
+                    push(
+                        mix.at[group, half, way], part.at[group, half, 2 + way],
+                        send.at[4], recv.at[4 + group], cross[half]((2 * sign) % RING),
                     )
                 )
 
@@ -292,8 +323,10 @@
     relay(3, 1, 1)
     add_blocks((3, 5), 1)
     finish(1)
+    combine(0)
     drain(recv.at[3], hubs.at[pl.ds(0, 4)])
     lax.fori_loop(0, 8, hub_block, 0, unroll=True)
+    combine(1)
 
     product = jnp.zeros((SEEDS, 2 * LANES), jnp.float32)
     for group in range(2):
@@ -302,8 +335,8 @@
         for half in range(2):
             top = half * LANES + group * WIDE
             total = tot[top : top + WIDE] + pacc[half, spot[half], group]
-            for step in range(1, RING):
-                total = total + part[group, half, step - 1]
+            for source in range(4):
+                total = total + part[group, half, source]
             lines.append(total)
         mean = jnp.transpose(jnp.concatenate(lines, axis=0) / taken[...])
         parts = [weight[half * LANES + group * WIDE : half * LANES + (group + 1) * WIDE] for half in range(2)]
@@ -314,7 +347,8 @@
     drain(send.at[0], ag.at[:, pl.ds(0, RING - 1)])
     drain(send.at[1], meta_tx.at[:, pl.ds(0, RING - 1)])
     drain(send.at[2], hubs.at[pl.ds(0, 7)])
-    drain(send.at[3], part)
+    drain(send.at[3], far)
+    drain(send.at[4], part)
 
 
 def local(features, seed_self, hub_ids, requests, counts, neighbors, weight, out_bias):
@@ -343,12 +377,15 @@
             pltpu.VMEM((2, RING, 2 * LANES), jnp.int32),
             pltpu.VMEM((2, RING, 4, LANES, 2 * LANES), jnp.bfloat16),
             pltpu.VMEM((2, RING, 2, WIDE, LANES), jnp.float32),
-            pltpu.VMEM((2, 2, RING - 1, WIDE, LANES), jnp.float32),
+            pltpu.VMEM((2, 2, 4, WIDE, LANES), jnp.float32),
+            pltpu.VMEM((2, 2, 2, WIDE + WIDE // 2, LANES), jnp.float32),
+            pltpu.VMEM((2, 2, 2, WIDE, LANES), jnp.float32),
             pltpu.VMEM((2 * XS, 2 * LANES, LANES), jnp.float32),
             pltpu.VMEM((2 * LANES, LANES), jnp.float32),
             pltpu.VMEM((1, LANES), jnp.float32),
-            dma((4,)),
+            dma((5,)),
             dma((6,)),
+            dma((2, 2)),
             dma((2, 4, 2, 2)),
             pltpu.SemaphoreType.REGULAR((2, 2)),
         ],

time: 51.5 us -> 49.6 us (0.963)
  the two profiles are of different devices: /device:TPU:6 before, /device:TPU:8 now
where the time goes in v6:
time: 49.6 us; the launch traced here: 49.5 us
  Pallas kernels  48.8 us (98%)
  local copies, waits for them, and re-layouts  0.66 us (1%)
    pallas_call x1, Pallas kernels, local(): pl.pallas_call(kernel, out_shape=jax.ShapeDtypeStruct((SEEDS, 2 * LANES),...  48.8 us

profile of v6, /device:TPU:8, one launch (start us, length us, event | category | flops | bytes accessed | tf_op | source)
XLA Modules:
  0.0 49.5 jit_solution(13401217402015442815)
XLA Ops:
  0.0 48.8 %sage.1 = f32[128,256]{1,0:T(8,128)S(1)} custom-call(f32[512,256]{1,0:T(8,128)} %feat_in.1, f32[128,256]{1,0:T(8,128)} %own_in.1, s32[1,128]{1,0:T(1,128)} %bitcast.7, s32[32,64]{1,0:T(8,128)} %bitcast.4, s32[64]{0:T(128)} %counts_in.1, s32[15,128]{1,0:T(8,128)} %bitcast.5, f32[256,256]{1,0:T(8,128)} %weight_in.1, f32[1,256]{1,0:T(1,128)} %bitcast.6), custom_call_target="tpu_custom_call" | custom-call | tf_op jit(solution)/shard_map/sage/pallas_call | solution.py:358
  48.9 0.7 %copy.10 = f32[128,256]{1,0:T(8,128)} copy(f32[128,256]{1,0:T(8,128)S(1)} %sage.1) | data formatting | bytes 262144

commit v7 on v6

--- a/solution.py
+++ b/solution.py
@@ -18,6 +18,7 @@
 CHUNKS = 4
 LANES = 128
 WIDE = 64
+META = 18
 
 
 def split(values):
@@ -132,19 +133,19 @@
     codes = jnp.where(live, codes, -1)
     taken[...] = 1.0 + jnp.sum(live.astype(jnp.float32), axis=0, keepdims=True)
     req[...] = jnp.transpose(req_v[...])
-    lane = lax.broadcasted_iota(jnp.int32, (RING, LANES), 1) // CAP
+    packed = jnp.concatenate([req[pl.ds(p, 2 * RING, stride=4)] for p in range(4)], axis=1)
+    upper, lower = (
+        jnp.concatenate([req[(4 * h + p) * RING : (4 * h + p + 1) * RING] for p in range(4)], axis=1) for h in range(2)
+    )
+    for place in range(RING):
+        for half in range(2):
+            meta_tx[half, place, 0:16] = codes
+        meta_tx[0, place, 16:18] = packed[2 * place : 2 * place + 2]
+        meta_tx[1, place, 16:17] = upper[place : place + 1]
+        meta_tx[1, place, 17:18] = lower[place : place + 1]
     for half in range(2):
-        for place in range(RING):
-            if half == 0:
-                lists = req[place * RING : (place + 1) * RING]
-            else:
-                lists = req[pl.ds(place, RING, stride=RING)]
-            lists = jnp.concatenate([lists] * 4, axis=1)
-            meta_tx[half, place, 0:16] = codes
-            meta_tx[half, place, 16:24] = jnp.where(lane == spot[half] % 4, lists, 0)
         meta_rx[half, spot[half], 0:16] = codes
-    for half in range(2):
-        meta_rx[half, spot[half], 16:24] = meta_tx[half, spot[half], 16:24]
+        meta_rx[half, spot[half], 16:18] = meta_tx[half, spot[half], 16:18]
 
     for hop in range(3):
         for way in range(2):
@@ -158,7 +159,7 @@
         for half in range(2):
             place = (spot[half] + step) % RING
             copy = push(
-                meta_tx.at[half, place], meta_rx.at[half, spot[half]],
+                meta_tx.at[half, place, pl.ds(0, META)], meta_rx.at[half, spot[half], pl.ds(0, META)],
                 send.at[1], recv.at[0], cross[half](step),
             )
             launch(copy)
@@ -241,11 +242,18 @@
 
     relay(1, 0, 0)
     relay(1, 0, 1)
-    drain(recv.at[0], meta_rx.at[:, pl.ds(0, RING - 1)])
+    drain(recv.at[0], meta_rx.at[:, pl.ds(0, RING - 1), pl.ds(0, META)])
+    set_of = lax.broadcasted_iota(jnp.int32, (2, LANES), 1) // CAP
     for half in range(2):
         for group in range(2):
-            tiles = [meta_rx[half, 4 * group + k, 16:24] for k in range(4)]
-            ids[half, :, group * LANES : (group + 1) * LANES] = tiles[0] + tiles[1] + tiles[2] + tiles[3]
+            lists = [meta_rx[half, 4 * group + k, 16:18] for k in range(4)]
+            for p in range(4):
+                row = jnp.zeros((2, LANES), jnp.int32)
+                for k in range(4):
+                    taken_set = jnp.where(set_of == p, lists[k], 0)
+                    row = row + (pltpu.roll(taken_set, ((k - p) % 4) * CAP, 1) if k != p else taken_set)
+                ids[half, p : p + 1, group * LANES : (group + 1) * LANES] = row[0:1]
+                ids[half, 4 + p : 5 + p, group * LANES : (group + 1) * LANES] = row[1:2]
     lay_counts((0,))
     add_blocks((0,), 0)
     add_blocks((0,), 1)
@@ -345,7 +353,7 @@
         )
     out[...] = jnp.maximum(product + bias[...], 0.0)
     drain(send.at[0], ag.at[:, pl.ds(0, RING - 1)])
-    drain(send.at[1], meta_tx.at[:, pl.ds(0, RING - 1)])
+    drain(send.at[1], meta_tx.at[:, pl.ds(0, RING - 1), pl.ds(0, META)])
     drain(send.at[2], hubs.at[pl.ds(0, 7)])
     drain(send.at[3], far)
     drain(send.at[4], part)

time: 49.6 us -> 48.7 us (0.982)
  the two profiles are of different devices: /device:TPU:8 before, /device:TPU:6 now
where the time goes in v7:
time: 48.7 us; the launch traced here: 48.5 us
  Pallas kernels  47.9 us (98%)
  local copies, waits for them, and re-layouts  0.66 us (1%)
    pallas_call x1, Pallas kernels, local(): pl.pallas_call(kernel, out_shape=jax.ShapeDtypeStruct((SEEDS, 2 * LANES),...  47.9 us

profile of v7, /device:TPU:6, one launch (start us, length us, event | category | flops | bytes accessed | tf_op | source)
XLA Modules:
  0.0 48.5 jit_solution(4482831484990015876)
XLA Ops:
  0.0 47.9 %sage.1 = f32[128,256]{1,0:T(8,128)S(1)} custom-call(f32[512,256]{1,0:T(8,128)} %feat_in.1, f32[128,256]{1,0:T(8,128)} %own_in.1, s32[1,128]{1,0:T(1,128)} %bitcast.7, s32[32,64]{1,0:T(8,128)} %bitcast.4, s32[64]{0:T(128)} %counts_in.1, s32[15,128]{1,0:T(8,128)} %bitcast.5, f32[256,256]{1,0:T(8,128)} %weight_in.1, f32[1,256]{1,0:T(1,128)} %bitcast.6), custom_call_target="tpu_custom_call" | custom-call | tf_op jit(solution)/shard_map/sage/pallas_call | solution.py:366
  47.9 0.7 %copy.10 = f32[128,256]{1,0:T(8,128)} copy(f32[128,256]{1,0:T(8,128)S(1)} %sage.1) | data formatting | bytes 262144

commit v8 on v7

--- a/solution.py
+++ b/solution.py
@@ -242,6 +242,7 @@
 
     relay(1, 0, 0)
     relay(1, 0, 1)
+    relay(1, 1, 0)
     drain(recv.at[0], meta_rx.at[:, pl.ds(0, RING - 1), pl.ds(0, META)])
     set_of = lax.broadcasted_iota(jnp.int32, (2, LANES), 1) // CAP
     for half in range(2):
@@ -257,7 +258,6 @@
     lay_counts((0,))
     add_blocks((0,), 0)
     add_blocks((0,), 1)
-    relay(1, 1, 0)
     relay(1, 1, 1)
     drain(recv.at[1], hubs.at[pl.ds(0, 2)])
     low, high = pl.ds(0, LANES), pl.ds(LANES, LANES)

time: 48.7 us -> 48.8 us (level); the launches traced: 48.5 us -> 48.1 us
  Pallas kernels: 47.9 us -> 47.4 us
where the time goes in v8:
time: 48.8 us; the launch traced here: 48.1 us
  Pallas kernels  47.4 us (97%)
  local copies, waits for them, and re-layouts  0.66 us (1%)
    pallas_call x1, Pallas kernels, local(): pl.pallas_call(kernel, out_shape=jax.ShapeDtypeStruct((SEEDS, 2 * LANES),...  47.4 us

profile of v8, /device:TPU:6, one launch (start us, length us, event | category | flops | bytes accessed | tf_op | source)
XLA Modules:
  0.0 48.1 jit_solution(4286018626757003403)
XLA Ops:
  0.0 47.4 %sage.1 = f32[128,256]{1,0:T(8,128)S(1)} custom-call(f32[512,256]{1,0:T(8,128)} %feat_in.1, f32[128,256]{1,0:T(8,128)} %own_in.1, s32[1,128]{1,0:T(1,128)} %bitcast.7, s32[32,64]{1,0:T(8,128)} %bitcast.4, s32[64]{0:T(128)} %counts_in.1, s32[15,128]{1,0:T(8,128)} %bitcast.5, f32[256,256]{1,0:T(8,128)} %weight_in.1, f32[1,256]{1,0:T(1,128)} %bitcast.6), custom_call_target="tpu_custom_call" | custom-call | tf_op jit(solution)/shard_map/sage/pallas_call | solution.py:366
  47.4 0.7 %copy.10 = f32[128,256]{1,0:T(8,128)} copy(f32[128,256]{1,0:T(8,128)S(1)} %sage.1) | data formatting | bytes 262144
